TPU v7x, 32 devices: a whole 2x2x4 slice. The times are simulated.
32 devices in a mesh: gx: 4 (over y, x), gy: 4 (over z), gz: 2 (over core).
Axes of the slice: x: 2, y: 2, z: 4, core: 2. Of those that a mesh axis runs over, the one named last changes fastest.
Arguments:
- surface_ids: int32 [256, 256, 256], P('gx', 'gy', 'gz'), may hold values from 0 to 256, as said below
- class_map: int32 [256, 256, 256], P('gx', 'gy', 'gz'), may hold values from 0 to 3
- conductivity: float32 [256, 256, 256], P('gx', 'gy', 'gz'), may hold values from 0.5 to 2
- normals: float32 [3, 256], replicated, may hold values from -9 to 9
- class_table: float32 [4], replicated, may hold values from 0.25 to 1
Outputs:
- distance: float32 [256, 256, 256], P('gx', 'gy', 'gz')
Inputs may be any that keep to these rules, and one draw needn't show every extreme that they name: `surface_ids`: 0 marks a cell without a source and k a cell of patch k; each cell holds a source with probability one quarter, of a patch drawn evenly.
All inputs are finite; a program needn't handle non-finite values.
Results may differ from a plain program's by a relative error of at most 0.0003.
Values sent between devices are 32-bit elements; how exact they have to be, the bound alone decides.
No kernel may reach another device: no remote copies, remote signals or barrier semaphores. Data moves between devices by JAX's collectives and lax.ppermute only.
A program may use at most 128 MiB of HBM per device.

v0:
```python
import jax
import jax.numpy as jnp
from jax import lax
from jax.sharding import PartitionSpec as P

N = 256
STEPS = 8
CLASSES = 4


time_step = 0.08
norm_floor = 0.5
offsets = ((1, 0, 0), (-1, 0, 0), (0, 1, 0), (0, -1, 0), (0, 0, 1), (0, 0, -1))


def padded_2(cells, sides, width):
    for axis, dim in sides:
        count = lax.axis_size(axis)
        ends = count - 1
        head = lax.slice_in_dim(cells, 0, width, axis=dim)
        tail = lax.slice_in_dim(cells, cells.shape[dim] - width, cells.shape[dim], axis=dim)
        cells = jnp.concatenate(
            [
                lax.ppermute(tail, axis, [(i, (i + 1) % count) for i in range(ends)]),
                cells,
                lax.ppermute(head, axis, [((i + 1) % count, i) for i in range(ends)]),
            ],
            axis=dim,
        )
    return cells


def shifted(padded, offset):
    extent = padded.shape[-3:]
    return padded[
        ...,
        1 + offset[0] : extent[0] - 1 + offset[0],
        1 + offset[1] : extent[1] - 1 + offset[1],
        1 + offset[2] : extent[2] - 1 + offset[2],
    ]


def diffuse(padded, root_field):
    center = shifted(padded, (0, 0, 0))
    middle = shifted(root_field, (0, 0, 0))
    inflow = jnp.zeros_like(center)
    for offset in offsets:
        inflow = inflow + shifted(root_field, offset) * (shifted(padded, offset) - center)
    return center + time_step * middle * inflow


def cosine_table(length):
    wave_number = jnp.arange(length, dtype=jnp.float32)[:, None]
    sample = jnp.arange(length, dtype=jnp.float32)[None, :]
    factor = jnp.where(wave_number == 0, jnp.sqrt(1.0 / length), jnp.sqrt(2.0 / length))
    return factor * jnp.cos(jnp.pi * wave_number * (2.0 * sample + 1.0) / (2.0 * length))


def eigen_values(length):
    wave_number = jnp.arange(length, dtype=jnp.float32)
    return 2.0 - 2.0 * jnp.cos(jnp.pi * wave_number / length)


def normalize(heat_field):
    magnitude = jnp.sqrt(
        heat_field[0] * heat_field[0]
        + heat_field[1] * heat_field[1]
        + heat_field[2] * heat_field[2]
    )
    return heat_field / jnp.maximum(magnitude, norm_floor)


def along_last(values, matrix):
    return jnp.dot(values, matrix, precision=lax.Precision.HIGHEST)


def lookup_sources(surface_ids, lookup_table):
    cell_count = surface_ids.size
    block_cells = min(cell_count, 8192)
    block_count = cell_count // block_cells
    entries = lookup_table.shape[1]
    blocked_ids = surface_ids.reshape(block_count, block_cells)
    choices_row = jnp.arange(entries, dtype=jnp.int32)[None, :]

    def one_block(block_ids):
        one_hot = (block_ids[:, None] == choices_row).astype(jnp.float32)
        return jnp.einsum("ck,nk->cn", lookup_table, one_hot, precision=lax.Precision.HIGHEST)

    values = lax.map(one_block, blocked_ids)
    return values.transpose(1, 0, 2).reshape((3,) + surface_ids.shape)


def per_device(surface_ids, class_map, conductivity, normals, class_table):
    width_x, width_y, width_z = surface_ids.shape
    lookup_table = jnp.concatenate([jnp.zeros((3, 1), jnp.float32), normals], axis=1)
    source = lookup_sources(surface_ids, lookup_table)
    class_value = jnp.zeros(class_map.shape, jnp.float32)
    for class_index in range(CLASSES):
        class_value = class_value + jnp.where(
            class_map == class_index, class_table[class_index], 0.0
        )
    root_field = jnp.sqrt(class_value * conductivity)
    heat_field = source
    rim_root = padded_2(root_field, (("gx", 0), ("gy", 1), ("gz", 2)), 1)
    for step_index in range(STEPS):
        padded = padded_2(heat_field, (("gx", 1), ("gy", 2), ("gz", 3)), 1)
        heat_field = diffuse(padded, rim_root)
    unit_field = normalize(heat_field)
    faces_x = padded_2(unit_field[0], (("gx", 0),), 1)
    faces_y = padded_2(unit_field[1], (("gy", 1),), 1)
    faces_z = padded_2(unit_field[2], (("gz", 2),), 1)
    part_x = 0.5 * (faces_x[2:] - faces_x[:-2])
    part_y = 0.5 * (faces_y[:, 2:] - faces_y[:, :-2])
    part_z = 0.5 * (faces_z[:, :, 2:] - faces_z[:, :, :-2])
    divergence = part_x + part_y + part_z
    cosine = cosine_table(N)
    forward = cosine.T
    narrow = lax.axis_size("gz")
    wide_count = lax.axis_size("gy")
    group_count = lax.axis_size("gx") * narrow
    x_rows = width_x // narrow
    kz_rows = N // wide_count
    ky_rows = N // group_count
    pencil = lax.all_to_all(divergence, "gz", split_axis=0, concat_axis=2, tiled=True)
    pencil = along_last(pencil.reshape(x_rows * width_y, N), forward)
    packed = (
        pencil.reshape(x_rows, width_y, wide_count, kz_rows)
        .transpose(2, 0, 1, 3)
        .reshape(wide_count, x_rows, width_y * kz_rows)
    )
    packed = lax.all_to_all(packed, "gy", split_axis=0, concat_axis=0, tiled=True)
    pencil = (
        packed.reshape(wide_count, x_rows, width_y, kz_rows)
        .transpose(1, 3, 0, 2)
        .reshape(x_rows * kz_rows, N)
    )
    pencil = along_last(pencil, forward)
    packed = (
        pencil.reshape(x_rows, kz_rows, group_count, ky_rows)
        .transpose(2, 0, 1, 3)
        .reshape(group_count, x_rows, kz_rows * ky_rows)
    )
    packed = lax.all_to_all(packed, ("gx", "gz"), split_axis=0, concat_axis=0, tiled=True)
    pencil = (
        packed.reshape(group_count, x_rows, kz_rows, ky_rows)
        .transpose(2, 3, 0, 1)
        .reshape(kz_rows * ky_rows, N)
    )
    pencil = along_last(pencil, forward)
    spectra = eigen_values(N)
    group_index = lax.axis_index("gx") * narrow + lax.axis_index("gz")
    spectra_z = lax.dynamic_slice_in_dim(spectra, lax.axis_index("gy") * kz_rows, kz_rows)
    spectra_y = lax.dynamic_slice_in_dim(spectra, group_index * ky_rows, ky_rows)
    screen = 4.0 / (N * N)
    divisor = spectra[None, None, :] + spectra_y[None, :, None] + spectra_z[:, None, None] + screen
    pencil = -pencil / divisor.reshape(kz_rows * ky_rows, N)
    pencil = along_last(pencil, cosine)
    packed = (
        pencil.reshape(kz_rows, ky_rows, group_count, x_rows)
        .transpose(2, 3, 0, 1)
        .reshape(group_count, x_rows, kz_rows * ky_rows)
    )
    packed = lax.all_to_all(packed, ("gx", "gz"), split_axis=0, concat_axis=0, tiled=True)
    pencil = (
        packed.reshape(group_count, x_rows, kz_rows, ky_rows)
        .transpose(1, 2, 0, 3)
        .reshape(x_rows * kz_rows, N)
    )
    pencil = along_last(pencil, cosine)
    packed = (
        pencil.reshape(x_rows, kz_rows, wide_count, width_y)
        .transpose(2, 0, 3, 1)
        .reshape(wide_count, x_rows, width_y * kz_rows)
    )
    packed = lax.all_to_all(packed, "gy", split_axis=0, concat_axis=0, tiled=True)
    pencil = (
        packed.reshape(wide_count, x_rows, width_y, kz_rows)
        .transpose(1, 2, 0, 3)
        .reshape(x_rows * width_y, N)
    )
    pencil = along_last(pencil, cosine).reshape(x_rows, width_y, N)
    return lax.all_to_all(pencil, "gz", split_axis=2, concat_axis=0, tiled=True)


def solution(mesh):
    in_specs = (P("gx", "gy", "gz"), P("gx", "gy", "gz"), P("gx", "gy", "gz"), P(), P())
    out_specs = P("gx", "gy", "gz")
    return jax.shard_map(
        per_device, mesh=mesh, in_specs=in_specs, out_specs=out_specs, check_vma=False
    )
```

profile of v0, /device:TPU:0, one launch (start us, length us, event | category | flops | bytes accessed | tf_op | source)
XLA Modules:
  0.0 1496.9 jit_solution(10147376568636349496)
XLA Ops:
  1.5 6.1 broadcast_multiply_fusion
  19.9 285.5 %while.11 = (s32[]{:T(128)}, f32[64,3,8192]{2,1,0:T(4,128)}, s32[64,8192]{1,0:T(8,128)}, f32[3,257]{1,0:T(4,128)S(1)}, s32[]{:T(128)}) while((s32[]{:T(128)}, f32[64,3,8192]{2,1,0:T(4,128)}, s32[64,8192]{1,0:T(8,128)}, f32[3,257]{1,0:T(4,128)S(1)}, s32[]{:T(128)}) %tuple.67), condition=%wide.region_1.2_spmd.clone, body=%wide.region_0.1_spmd.clone.sunk | while | flops 77897728 | bytes 233037 | solution.py:89
  305.4 11.3 reshape.214
  331.8 6.5 copy.203
  372.6 12.4 fusion.232
  399.4 15.9 %pad_maximum_fusion.147 = (f32[64,64,128]{1,0,2:T(8,128)}, f32[64,64,128]{1,0,2:T(8,128)}) fusion(f32[66,66,1]{1,0,2:T(8,128)S(1)} %collective-permute-done.8, f32[66,1,128]{1,0,2:T(8,128)} %copy.149, f32[66,64,128]{1,0,2:T(8,128)} %copy.148, f32[66,1,128]{1,0,2:T(8,128)} %copy.147, f32[66,66,1]{1,0,2:T(8,128)S(1)} %collective-permute-done.10), kind=kLoop, calls=%fused_computation.305 | loop fusion | flops 3145728 | bytes 6459424 | tf_op jit(solution)/shard_map/concatenate | solution.py:22
  434.1 27.0 %fusion.141 = f32[3,64,64,128]{3,2,1,0:T(8,128)S(1)} fusion(f32[3,64,64,128]{3,2,1,0:T(8,128)} %copy.203, f32[3,66,66,1]{3,2,1,0:T(8,128)} %copy.155, f32[3,66,1,128]{3,2,1,0:T(1,128)S(1)} %collective-permute-done.5, f32[3,66,64,128]{3,2,1,0:T(8,128)} %copy-done.10, f32[3,66,1,128]{3,2,1,0:T(1,128)S(1)} %collective-permute-done.7, ...), kind=kLoop, calls=%fused_computation.278 | loop fusion | flops 45613056 | bytes 34254944 | tf_op jit(solution)/shard_map/add | solution.py:49
  482.7 12.4 fusion.231
  518.7 28.5 %fusion.122 = f32[3,64,64,128]{3,2,1,0:T(8,128)S(1)} fusion(f32[3,64,64,128]{3,2,1,0:T(8,128)} %copy-done.9, f32[3,66,66,1]{3,2,1,0:T(8,128)} %copy.159, f32[3,66,1,128]{3,2,1,0:T(1,128)S(1)} %collective-permute-done.14, f32[3,66,1,128]{3,2,1,0:T(1,128)S(1)} %collective-permute-done.15, f32[3,1,64,128]{3,2,1,0:T(8,128)S(1)} %collective-permute-done.12, ...), kind=kLoop, calls=%fused_computation.241 | loop fusion | flops 58195968 | bytes 27766880 | tf_op jit(solution)/shard_map/add | solution.py:49
  569.3 12.4 fusion.230
  605.4 28.5 %fusion.103 = f32[3,64,64,128]{3,2,1,0:T(8,128)S(1)} fusion(f32[3,64,64,128]{3,2,1,0:T(8,128)} %copy-done.4, f32[3,66,66,1]{3,2,1,0:T(8,128)} %copy.163, f32[3,66,1,128]{3,2,1,0:T(1,128)S(1)} %collective-permute-done.20, f32[3,66,1,128]{3,2,1,0:T(1,128)S(1)} %collective-permute-done.21, f32[3,1,64,128]{3,2,1,0:T(8,128)S(1)} %collective-permute-done.18, ...), kind=kLoop, calls=%fused_computation.204 | loop fusion | flops 58195968 | bytes 27766880 | tf_op jit(solution)/shard_map/add | solution.py:49
  635.2 5.8 collective-permute-start.25
  656.3 12.4 fusion.229
  692.4 28.5 %fusion.84 = f32[3,64,64,128]{3,2,1,0:T(8,128)S(1)} fusion(f32[3,64,64,128]{3,2,1,0:T(8,128)} %copy-done.5, f32[3,66,66,1]{3,2,1,0:T(8,128)} %copy.167, f32[3,66,1,128]{3,2,1,0:T(1,128)S(1)} %collective-permute-done.26, f32[3,66,1,128]{3,2,1,0:T(1,128)S(1)} %collective-permute-done.27, f32[3,1,64,128]{3,2,1,0:T(8,128)S(1)} %collective-permute-done.24, ...), kind=kLoop, calls=%fused_computation.167 | loop fusion | flops 58195968 | bytes 27766880 | tf_op jit(solution)/shard_map/add | solution.py:49
  722.2 5.8 collective-permute-start.31
  743.4 12.4 fusion.228
  779.4 28.5 %fusion.65 = f32[3,64,64,128]{3,2,1,0:T(8,128)S(1)} fusion(f32[3,64,64,128]{3,2,1,0:T(8,128)} %copy-done.6, f32[3,66,66,1]{3,2,1,0:T(8,128)} %copy.171, f32[3,66,1,128]{3,2,1,0:T(1,128)S(1)} %collective-permute-done.32, f32[3,66,1,128]{3,2,1,0:T(1,128)S(1)} %collective-permute-done.33, f32[3,1,64,128]{3,2,1,0:T(8,128)S(1)} %collective-permute-done.30, ...), kind=kLoop, calls=%fused_computation.130 | loop fusion | flops 58195968 | bytes 27766880 | tf_op jit(solution)/shard_map/add | solution.py:49
  809.2 5.8 collective-permute-start.37
  830.4 12.4 fusion.227
  866.4 28.5 %fusion.46 = f32[3,64,64,128]{3,2,1,0:T(8,128)S(1)} fusion(f32[3,64,64,128]{3,2,1,0:T(8,128)} %copy-done.7, f32[3,66,66,1]{3,2,1,0:T(8,128)} %copy.175, f32[3,66,1,128]{3,2,1,0:T(1,128)S(1)} %collective-permute-done.38, f32[3,66,1,128]{3,2,1,0:T(1,128)S(1)} %collective-permute-done.39, f32[3,1,64,128]{3,2,1,0:T(8,128)S(1)} %collective-permute-done.36, ...), kind=kLoop, calls=%fused_computation.93 | loop fusion | flops 58195968 | bytes 27766880 | tf_op jit(solution)/shard_map/add | solution.py:49
  896.3 5.8 collective-permute-start.43
  917.4 12.4 fusion.226
  953.4 28.5 %fusion.27 = f32[3,64,64,128]{3,2,1,0:T(8,128)S(1)} fusion(f32[3,64,64,128]{3,2,1,0:T(8,128)} %copy-done.8, f32[3,66,66,1]{3,2,1,0:T(8,128)} %copy.179, f32[3,66,1,128]{3,2,1,0:T(1,128)S(1)} %collective-permute-done.44, f32[3,66,1,128]{3,2,1,0:T(1,128)S(1)} %collective-permute-done.45, f32[3,1,64,128]{3,2,1,0:T(8,128)S(1)} %collective-permute-done.42, ...), kind=kLoop, calls=%fused_computation.56 | loop fusion | flops 58195968 | bytes 27766880 | tf_op jit(solution)/shard_map/add | solution.py:49
  983.3 5.8 collective-permute-start.49
  1004.4 12.4 fusion.225
  1040.9 30.8 %fusion.8 = f32[3,64,64,128]{3,2,1,0:T(8,128)} fusion(f32[3,64,64,128]{3,2,1,0:T(8,128)} %copy-done.3, f32[3,66,66,1]{3,2,1,0:T(8,128)} %copy.183, f32[3,66,1,128]{3,2,1,0:T(1,128)S(1)} %collective-permute-done.50, f32[3,66,1,128]{3,2,1,0:T(1,128)S(1)} %collective-permute-done.51, f32[3,1,64,128]{3,2,1,0:T(8,128)S(1)} %collective-permute-done.48, ...), kind=kLoop, calls=%fused_computation.19 | loop fusion | flops 58195968 | bytes 27766880 | tf_op jit(solution)/shard_map/add | solution.py:49
  1077.0 28.5 %broadcast_divide_fusion = f32[3,64,64,128]{3,2,1,0:T(8,128)} fusion(f32[64,64,128]{2,1,0:T(8,128)} %fusion.166, f32[3,64,64,128]{3,2,1,0:T(8,128)} %copy-done.3, f32[3,66,1,128]{3,2,1,0:T(1,128)S(1)} %collective-permute-done.50, f32[3,1,64,128]{3,2,1,0:T(8,128)S(1)} %collective-permute-done.48, f32[3,1,64,128]{3,2,1,0:T(8,128)S(1)} %collective-permute-done.49, ...), kind=kLoop, calls=%fused_computation.308 | loop fusion | flops 59768832 | bytes 29864032 | tf_op jit(solution)/shard_map/div | solution.py:70
  1105.5 6.0 slice_bitcast_fusion.2
  1132.8 5.8 collective-permute-start.55
  1142.7 6.1 fusion.159
  1160.1 7.0 convolution_bitcast_fusion.3
  1178.5 48.5 %all-to-all-done.1 = f32[4,32,4096]{2,1,0:T(8,128)S(1)} async-done(((f32[4,32,4096]{2,1,0:T(8,128)}), f32[4,32,4096]{2,1,0:T(8,128)S(1)}, u32[]{:S(2)}, u32[]{:S(2)}) %all-to-all-start.1) | async-done | bytes 2097184 | tf_op jit(solution)/shard_map/all_to_all | solution.py:131
  1239.4 6.9 convolution_bitcast_fusion.2
  1246.3 7.0 copy.191
  1253.3 7.5 reshape.199
  1268.5 24.5 %all-to-all-done.2 = f32[8,32,2048]{2,1,0:T(8,128)S(1)} async-done(((f32[8,32,2048]{2,1,0:T(8,128)}), f32[8,32,2048]{2,1,0:T(8,128)S(1)}, u32[]{:S(2)}, u32[]{:S(2)}) %all-to-all-start.2) | async-done | bytes 2097184 | tf_op jit(solution)/shard_map/all_to_all | solution.py:143
  1297.8 6.4 reshape.217
  1304.2 6.0 fusion.156
  1317.4 6.3 copy.193
  1327.5 26.5 %all-to-all-done.3 = f32[8,32,2048]{2,1,0:T(8,128)S(1)} async-done(((f32[8,32,2048]{2,1,0:T(8,128)}), f32[8,32,2048]{2,1,0:T(8,128)S(1)}, u32[]{:S(2)}, u32[]{:S(2)}) %all-to-all-start.3) | async-done | bytes 2097184 | tf_op jit(solution)/shard_map/all_to_all | solution.py:163
  1358.8 6.8 copy.194
  1365.6 17.9 %convolution_bitcast_fusion.1 = f32[4,32,64,64]{2,3,0,1:T(8,128)} fusion(f32[32,64,256,1]{1,2,3,0:T(8,128)} %bitcast.105, f32[4,64]{1,0:T(4,128)S(1)} %multiply_add_fusion.1, f32[256]{0:T(256)S(1)} %get-tuple-element.131, f32[256]{0:T(256)S(1)} %get-tuple-element.130), kind=kOutput, calls=%fused_computation.312 | convolution fusion | flops 1610809344 | bytes 4197376 | tf_op jit(solution)/shard_map/dot_general | solution.py:74
  1383.5 5.6 copy.196
  1392.6 49.1 %all_to_all.54 = f32[4,32,4096]{2,1,0:T(8,128)} all-to-all(f32[4,32,4096]{2,1,0:T(8,128)S(1)} %reshape.205), channel_id=1, replica_groups=mesh['gx'=4,'gy'=4,'gz'=2] {'gy'}, dimensions={0} | all-to-all | bytes 4194304 | tf_op jit(solution)/shard_map/all_to_all | solution.py:175
  1446.4 7.8 copy.197
  1462.4 5.6 copy.198
  1472.2 6.5 all_to_all.55
  1479.3 8.1 reduce
  (392 shorter events, 797.7 us)
Async XLA Ops:
  8.9 307.8 %collective-permute-start = (f32[1,64,128]{2,1,0:T(8,128)S(1)}, f32[1,64,128]{2,1,0:T(8,128)S(1)}, u32[]{:S(2)}, u32[]{:S(2)}) collective-permute-start(f32[1,64,128]{2,1,0:T(8,128)S(1)} %get-tuple-element.121), channel_id=1, source_target_pairs={{8,0},{16,8},{24,16},{9,1},{17,9},{25,17},{10,2},{18,10},{26,18},{... | collective-permute-start | bytes 98312 | tf_op jit(solution)/shard_map/ppermute | solution.py:26
  10.2 306.5 %collective-permute-start.2 = (f32[1,64,128]{2,1,0:T(8,128)S(1)}, f32[1,64,128]{2,1,0:T(8,128)S(1)}, u32[]{:S(2)}, u32[]{:S(2)}) collective-permute-start(f32[1,64,128]{2,1,0:T(8,128)S(1)} %get-tuple-element.120), channel_id=1, source_target_pairs={{0,8},{8,16},{16,24},{1,9},{9,17},{17,25},{2,10},{10,18},{18,26},{... | collective-permute-start | bytes 98312 | tf_op jit(solution)/shard_map/ppermute | solution.py:24
  319.9 23.2 %collective-permute-start.6 = (f32[66,1,128]{2,0,1:T(8,128)S(1)}, f32[66,1,128]{2,0,1:T(8,128)S(1)}, u32[]{:S(2)}, u32[]{:S(2)}) collective-permute-start(f32[66,1,128]{2,0,1:T(8,128)S(1)} %copy.208), channel_id=1, source_target_pairs={{0,2},{2,4},{4,6},{1,3},{3,5},{5,7},{8,10},{10,12},{12,14},{9,11},... | collective-permute-start | bytes 101384 | tf_op jit(solution)/shard_map/ppermute | solution.py:24
  323.9 22.3 %collective-permute-start.4 = (f32[66,1,128]{2,0,1:T(8,128)S(1)}, f32[66,1,128]{2,0,1:T(8,128)S(1)}, u32[]{:S(2)}, u32[]{:S(2)}) collective-permute-start(f32[66,1,128]{2,0,1:T(8,128)S(1)} %copy.207), channel_id=1, source_target_pairs={{2,0},{4,2},{6,4},{3,1},{5,3},{7,5},{10,8},{12,10},{14,12},{11,9},... | collective-permute-start | bytes 101384 | tf_op jit(solution)/shard_map/ppermute | solution.py:26
  326.2 26.7 %collective-permute-start.3 = (f32[3,1,64,128]{3,2,1,0:T(8,128)S(1)}, f32[3,1,64,128]{3,2,1,0:T(8,128)S(1)}, u32[]{:S(2)}, u32[]{:S(2)}) collective-permute-start(f32[3,1,64,128]{3,2,1,0:T(8,128)S(1)} %get-tuple-element.109), channel_id=1, source_target_pairs={{0,8},{8,16},{16,24},{1,9},{9,17},{17,25},{2,10},{10,18},{18,26},{... | collective-permute-start | bytes 294920 | tf_op jit(solution)/shard_map/ppermute | solution.py:24
  330.5 26.4 %collective-permute-start.1 = (f32[3,1,64,128]{3,2,1,0:T(8,128)S(1)}, f32[3,1,64,128]{3,2,1,0:T(8,128)S(1)}, u32[]{:S(2)}, u32[]{:S(2)}) collective-permute-start(f32[3,1,64,128]{3,2,1,0:T(8,128)S(1)} %get-tuple-element.108), channel_id=1, source_target_pairs={{8,0},{16,8},{24,16},{9,1},{17,9},{25,17},{10,2},{18,10},{26,18},{... | collective-permute-start | bytes 294920 | tf_op jit(solution)/shard_map/ppermute | solution.py:26
  350.1 49.3 %collective-permute-start.10 = (f32[66,66,1]{1,0,2:T(8,128)S(1)}, f32[66,66,1]{1,0,2:T(8,128)S(1)}, u32[]{:S(2)}, u32[]{:S(2)}) collective-permute-start(f32[66,66,1]{1,0,2:T(8,128)S(1)} %get-tuple-element.56), channel_id=1, source_target_pairs={{0,1},{2,3},{4,5},{6,7},{8,9},{10,11},{12,13},{14,15},{16,17},{18,... | collective-permute-start | bytes 52280 | tf_op jit(solution)/shard_map/ppermute | solution.py:24
  351.4 48.0 %collective-permute-start.8 = (f32[66,66,1]{1,0,2:T(8,128)S(1)}, f32[66,66,1]{1,0,2:T(8,128)S(1)}, u32[]{:S(2)}, u32[]{:S(2)}) collective-permute-start(f32[66,66,1]{1,0,2:T(8,128)S(1)} %get-tuple-element.55), channel_id=1, source_target_pairs={{1,0},{3,2},{5,4},{7,6},{9,8},{11,10},{13,12},{15,14},{17,16},{19,... | collective-permute-start | bytes 52280 | tf_op jit(solution)/shard_map/ppermute | solution.py:26
  357.1 11.4 collective-permute-start.5
  358.4 10.1 collective-permute-start.7
  390.0 34.9 %collective-permute-start.9 = (f32[3,66,66,1]{2,3,1,0:T(1,128)S(1)}, f32[3,66,66,1]{2,3,1,0:T(1,128)S(1)}, u32[]{:S(2)}, u32[]{:S(2)}) collective-permute-start(f32[3,66,66,1]{2,3,1,0:T(1,128)S(1)} %copy.151), channel_id=1, source_target_pairs={{1,0},{3,2},{5,4},{7,6},{9,8},{11,10},{13,12},{15,14},{17,16},{19,... | collective-permute-start | bytes 156824 | tf_op jit(solution)/shard_map/ppermute | solution.py:26
  396.3 33.1 %collective-permute-start.11 = (f32[3,66,66,1]{2,3,1,0:T(1,128)S(1)}, f32[3,66,66,1]{2,3,1,0:T(1,128)S(1)}, u32[]{:S(2)}, u32[]{:S(2)}) collective-permute-start(f32[3,66,66,1]{2,3,1,0:T(1,128)S(1)} %copy.154), channel_id=1, source_target_pairs={{0,1},{2,3},{4,5},{6,7},{8,9},{10,11},{12,13},{14,15},{16,17},{18,... | collective-permute-start | bytes 156824 | tf_op jit(solution)/shard_map/ppermute | solution.py:24
  462.4 7.4 collective-permute-start.13
  500.1 9.4 collective-permute-start.16
  506.4 7.7 collective-permute-start.17
  547.3 7.4 collective-permute-start.18
  548.6 7.6 collective-permute-start.19
  586.7 9.4 collective-permute-start.22
  593.1 7.7 collective-permute-start.23
  633.9 7.8 collective-permute-start.24
  635.2 8.0 collective-permute-start.25
  673.7 9.4 collective-permute-start.28
  680.1 7.7 collective-permute-start.29
  720.9 7.8 collective-permute-start.30
  722.2 8.0 collective-permute-start.31
  760.8 9.4 collective-permute-start.34
  767.1 7.7 collective-permute-start.35
  807.9 7.8 collective-permute-start.36
  809.2 8.0 collective-permute-start.37
  847.8 9.4 collective-permute-start.40
  854.1 7.7 collective-permute-start.41
  895.0 7.8 collective-permute-start.42
  896.3 8.0 collective-permute-start.43
  934.8 9.4 collective-permute-start.46
  941.1 7.7 collective-permute-start.47
  982.0 7.8 collective-permute-start.48
  983.3 8.0 collective-permute-start.49
  1021.8 9.8 collective-permute-start.52
  1028.2 8.1 collective-permute-start.53
  1117.3 15.4 %collective-permute-start.58 = (f32[64,64,1]{1,0,2:T(8,128)S(1)}, f32[64,64,1]{1,0,2:T(8,128)S(1)}, u32[]{:S(2)}, u32[]{:S(2)}) collective-permute-start(f32[64,64,1]{1,0,2:T(8,128)S(1)} %copy.184), channel_id=1, source_target_pairs={{1,0},{3,2},{5,4},{7,6},{9,8},{11,10},{13,12},{15,14},{17,16},{19,... | collective-permute-start | bytes 49160 | tf_op jit(solution)/shard_map/ppermute | solution.py:26
  1120.9 19.7 %collective-permute-start.59 = (f32[64,64,1]{1,0,2:T(8,128)S(1)}, f32[64,64,1]{1,0,2:T(8,128)S(1)}, u32[]{:S(2)}, u32[]{:S(2)}) collective-permute-start(f32[64,64,1]{1,0,2:T(8,128)S(1)} %copy.186), channel_id=1, source_target_pairs={{0,1},{2,3},{4,5},{6,7},{8,9},{10,11},{12,13},{14,15},{16,17},{18,... | collective-permute-start | bytes 49160 | tf_op jit(solution)/shard_map/ppermute | solution.py:24
  1125.0 17.7 %collective-permute-start.56 = (f32[64,1,128]{2,1,0:T(1,128)S(1)}, f32[64,1,128]{2,1,0:T(1,128)S(1)}, u32[]{:S(2)}, u32[]{:S(2)}) collective-permute-start(f32[64,1,128]{2,1,0:T(1,128)S(1)} %get-tuple-element.116), channel_id=1, source_target_pairs={{2,0},{4,2},{6,4},{3,1},{5,3},{7,5},{10,8},{12,10},{14,12},{11,9},... | collective-permute-start | bytes 98312 | tf_op jit(solution)/shard_map/ppermute | solution.py:26
  1126.3 16.4 %collective-permute-start.57 = (f32[64,1,128]{2,1,0:T(1,128)S(1)}, f32[64,1,128]{2,1,0:T(1,128)S(1)}, u32[]{:S(2)}, u32[]{:S(2)}) collective-permute-start(f32[64,1,128]{2,1,0:T(1,128)S(1)} %get-tuple-element.117), channel_id=1, source_target_pairs={{0,2},{2,4},{4,6},{1,3},{3,5},{5,7},{8,10},{10,12},{12,14},{9,11},... | collective-permute-start | bytes 98312 | tf_op jit(solution)/shard_map/ppermute | solution.py:24
  1131.5 11.2 collective-permute-start.54
  1132.8 9.9 collective-permute-start.55
  1173.5 53.4 %all-to-all-start.1 = ((f32[4,32,4096]{2,1,0:T(8,128)}), f32[4,32,4096]{2,1,0:T(8,128)S(1)}, u32[]{:S(2)}, u32[]{:S(2)}) async-start(f32[4,32,4096]{2,1,0:T(8,128)} %copy.189), calls=%async_computation.1 | async-start | bytes 4194304 | tf_op jit(solution)/shard_map/all_to_all | solution.py:131
  1260.8 32.1 %all-to-all-start.2 = ((f32[8,32,2048]{2,1,0:T(8,128)}), f32[8,32,2048]{2,1,0:T(8,128)S(1)}, u32[]{:S(2)}, u32[]{:S(2)}) async-start(f32[8,32,2048]{2,1,0:T(8,128)} %reshape.199), calls=%async_computation.2 | async-start | bytes 4194304 | tf_op jit(solution)/shard_map/all_to_all | solution.py:143
  1323.7 30.3 %all-to-all-start.3 = ((f32[8,32,2048]{2,1,0:T(8,128)}), f32[8,32,2048]{2,1,0:T(8,128)S(1)}, u32[]{:S(2)}, u32[]{:S(2)}) async-start(f32[8,32,2048]{2,1,0:T(8,128)} %copy.193), calls=%async_computation.3 | async-start | bytes 4194304 | tf_op jit(solution)/shard_map/all_to_all | solution.py:163
  (30 other events, 289.5 us)
where the time goes:
time: 1510 us; the launch traced here: 1500 us
  local copies, waits for them, and re-layouts  505 us (33%)
  other arithmetic  344 us (23%)
  matrix products  268 us (18%)
  starting transfers between devices  188 us (12%)
  waiting for transfers between devices  129 us (9%)
  blocking collectives  61.1 us (4%)
    add x8, other arithmetic, diffuse(): return center + time_step * middle * inflow  229 us
    dot_general x64, matrix products, one_block(): jnp.einsum('ck,nk->cn', lookup_table, one_hot, precision=lax.Precision.HI...  223 us
    slice x21, local copies, waits for them, and re-layouts, padded_2(): head = lax.slice_in_dim(cells, 0, width, axis=dim)  147 us
    ppermute x30, starting transfers between devices, padded_2(): lax.ppermute(tail, axis, [(i, (i + 1) % count) for i in range(ends)])  135 us
    dynamic_slice x64, local copies, waits for them, and re-layouts, lookup_sources(): values = lax.map(one_block, blocked_ids)  62.4 us
    concatenate x18, other arithmetic, padded_2(): jnp.concatenate([lax.ppermute(tail, axis, [(i, (i + 1) % count) for i in...  58.6 us
    all_to_all x2, waiting for transfers between devices, per_device(): lax.all_to_all(packed, ('gx', 'gz'), split_axis=0, concat_axis=0, tiled=T...  51 us
    all_to_all x1, blocking collectives, per_device(): lax.all_to_all(packed, 'gy', split_axis=0, concat_axis=0, tiled=True)  49.1 us
  transfers between devices with their start and end apart: 63, of which 31 were waited for; matrix products, arithmetic and copies ran while one was open for 31% of the time, Pallas kernels for 0%

commit v1 on v0

v1 whole, which is shorter than its diff:
```python
import functools

import jax
import jax.numpy as jnp
import numpy as np
from jax import lax
from jax.experimental import pallas as pl
from jax.experimental.pallas import tpu as pltpu
from jax.sharding import PartitionSpec as P

STEPS = 8
TIME_STEP = 0.08
NORM_FLOOR = 0.5
LANES = 128
SUBLANES = 8
HALO = STEPS + 1
PAD = 2 * SUBLANES
HIGHEST = lax.Precision.HIGHEST


def cosine_table(length):
    f32 = np.float32
    wave = np.arange(length, dtype=f32)[:, None]
    sample = np.arange(length, dtype=f32)[None, :]
    factor = np.where(wave == 0, np.sqrt(f32(1.0 / length)), np.sqrt(f32(2.0 / length)))
    angle = f32(np.pi) * wave * (f32(2.0) * sample + f32(1.0)) / f32(2.0 * length)
    return (factor * np.cos(angle)).astype(f32)


def eigen_values(length):
    wave = np.arange(length, dtype=np.float32)
    return (np.float32(2.0) - np.float32(2.0) * np.cos(np.float32(np.pi) * wave / np.float32(length))).astype(
        np.float32
    )


def exact_table(length):
    wave = np.arange(length, dtype=np.float64)[:, None]
    sample = np.arange(length, dtype=np.float64)[None, :]
    factor = np.where(wave == 0, np.sqrt(1.0 / length), np.sqrt(2.0 / length))
    return factor * np.cos(np.pi * wave * (2.0 * sample + 1.0) / (2.0 * length))


def dot(a, b):
    return jnp.dot(a, b, precision=HIGHEST, preferred_element_type=jnp.float32)


def dot_nt(a, b):
    return lax.dot_general(
        a, b, (((1,), (1,)), ((), ())), precision=HIGHEST, preferred_element_type=jnp.float32
    )


def halves(values):
    high = values.astype(jnp.bfloat16)
    return high, (values - high.astype(jnp.float32)).astype(jnp.bfloat16)


def table_halves(table):
    table = np.asarray(table, np.float32)
    high = table.astype(jnp.bfloat16)
    return jnp.asarray(np.stack([high, (table - high.astype(np.float32)).astype(jnp.bfloat16)]))


def product(a, b, contract):
    def part(x, y):
        return lax.dot_general(x, y, (contract, ((), ())), preferred_element_type=jnp.float32)

    return part(a[0], b[0]) + (part(a[0], b[1]) + part(a[1], b[0]))


NN = ((1,), (0,))
NT = ((1,), (1,))


def z_neighbours(tiles, first, last):
    below = [pltpu.roll(t, 1, 1) for t in tiles]
    above = [pltpu.roll(t, LANES - 1, 1) for t in tiles]
    count = len(tiles)
    down = [jnp.where(first, below[h - 1] if h else 0.0, below[h]) for h in range(count)]
    up = [jnp.where(last, above[h + 1] if h + 1 < count else 0.0, above[h]) for h in range(count)]
    return up, down


def diffuse_kernel(
    own_ref, west_ref, east_ref, south_ref, north_ref, sw_ref, se_ref, nw_ref, ne_ref, table_ref, cosine_ref,
    out_ref, field_ref, va, vb, keep_ref, gain_ref, za, zb, sems, *, dims
):
    tiles, planes, rows, own_x, own_y, pack, groups = dims
    span = own_y + 2 * SUBLANES
    chunk = pl.ds(SUBLANES, span)
    lane = lax.broadcasted_iota(jnp.int32, (span, LANES), 1)
    first, last = lane == 0, lane == LANES - 1
    table_blocks = table_ref.shape[1]
    every = range(tiles)
    own_rows = pl.ds(PAD, own_y)

    copies = [
        pltpu.make_async_copy(
            ref, field_ref.at[:, :, pl.ds(start, size), own_rows, :], sems.at[n]
        )
        for n, (ref, start, size) in enumerate(
            ((west_ref, 0, HALO), (own_ref, HALO, own_x), (east_ref, HALO + own_x, HALO))
        )
    ]
    for copy in copies:
        copy.start()

    def rim(ref, begin, above):
        def one(x, carry):
            for h in every:
                for f in range(2):
                    if above:
                        eight, single, at = x * HALO, x * HALO + SUBLANES, PAD + own_y
                        far = at + SUBLANES
                    else:
                        eight, single, at = x * HALO + 1, x * HALO, SUBLANES
                        far = at - 1
                    field_ref[h, f, begin + x, pl.ds(at, SUBLANES), :] = ref[
                        h, f, pl.ds(eight, SUBLANES), :
                    ]
                    field_ref[h, f, begin + x, pl.ds(far, 1), :] = ref[h, f, pl.ds(single, 1), :]
            return carry

        lax.fori_loop(0, ref.shape[2] // HALO, one, 0)

    rim(sw_ref, 0, False)
    rim(south_ref, HALO, False)
    rim(se_ref, HALO + own_x, False)
    rim(nw_ref, 0, True)
    rim(north_ref, HALO, True)
    rim(ne_ref, HALO + own_x, True)
    for copy in copies:
        copy.wait()

    row = lax.broadcasted_iota(jnp.int32, (SUBLANES, LANES), 0)

    def spread(x):
        for y in range(rows // SUBLANES):
            at = pl.ds(y * SUBLANES, SUBLANES)
            for h in every:
                ids = field_ref[h, 0, x, at, :]
                root = field_ref[h, 1, x, at, :]
                if y == 0 or y == rows // SUBLANES - 1:
                    inside = row == (SUBLANES - 1 if y == 0 else 0)
                    ids = jnp.where(inside, ids, 0.0)
                    root = jnp.where(inside, root, 0.0)
                ids = ids.astype(jnp.int32)
                low = (ids - 1) & (LANES - 1)
                high = (ids - 1) >> (LANES.bit_length() - 1)
                for c in range(3):
                    value = jnp.zeros((SUBLANES, LANES), jnp.float32)
                    for k in range(table_blocks):
                        found = jnp.take_along_axis(table_ref[c, k], low, axis=1)
                        value = jnp.where(high == k, found, value)
                    va[c, h, x, at, :] = value * root

    def coefficients(x):
        one = jnp.minimum(x, 1)
        mid = [field_ref[h, 1, x, chunk, :] for h in every]
        up, down = z_neighbours(mid, first, last)
        for h in every:
            total = (
                (field_ref[h, 1, x + 1, chunk, :] + field_ref[h, 1, x - 1, chunk, :])
                + (
                    field_ref[h, 1, x, pl.ds(SUBLANES + one, span), :]
                    + field_ref[h, 1, x, pl.ds(SUBLANES - one, span), :]
                )
                + (up[h] + down[h])
            )
            scaled = TIME_STEP * mid[h]
            keep_ref[h, x, chunk, :] = 1.0 - scaled * total
            gain_ref[h, x, chunk, :] = scaled * mid[h]

    def prepare(x, carry):
        spread(x)
        coefficients(x)
        return carry

    spread(0)
    lax.fori_loop(1, planes - 1, prepare, 0)
    spread(planes - 1)

    tile_lane = lax.broadcasted_iota(jnp.int32, (SUBLANES, LANES), 1)
    tile_first, tile_last = tile_lane == 0, tile_lane == LANES - 1

    def along_z(source, x, y, kept):
        at = pl.ds(SUBLANES * (y + 1), SUBLANES)
        for c in range(3):
            up, down = z_neighbours([source[c, h, x, at, :] for h in every], tile_first, tile_last)
            for h in every:
                kept[c, h, pl.ds(y * SUBLANES, SUBLANES), :] = up[h] + down[h]

    def update(source, target, x, y, kept, one):
        base = SUBLANES * (y + 1)
        at = pl.ds(base, SUBLANES)
        for h in every:
            keep, gain = keep_ref[h, x, at, :], gain_ref[h, x, at, :]
            for c in range(3):
                total = (
                    (source[c, h, x + 1, at, :] + source[c, h, x - 1, at, :])
                    + (
                        source[c, h, x, pl.ds(base + one, SUBLANES), :]
                        + source[c, h, x, pl.ds(base - one, SUBLANES), :]
                    )
                    + kept[c, h, pl.ds(y * SUBLANES, SUBLANES), :]
                )
                target[c, h, x, at, :] = keep * source[c, h, x, at, :] + gain * total

    def sweep(source, target, begin):
        for y in range(span // SUBLANES):
            along_z(source, begin, y, za)

        def two_planes(pair, carry):
            x = begin + 2 * pair
            one = jnp.minimum(x, 1)
            for y in range(span // SUBLANES):
                update(source, target, x, y, za, one)
                along_z(source, x + 1, y, zb)
            for y in range(span // SUBLANES):
                update(source, target, x + 1, y, zb, one)
                along_z(source, x + 2, y, za)
            return carry

        lax.fori_loop(0, planes // 2 - begin, two_planes, 0)

    def two_steps(pair, carry):
        sweep(va, vb, 2 * pair + 1)
        sweep(vb, va, 2 * pair + 2)
        return carry

    lax.fori_loop(0, STEPS // 2, two_steps, 0)

    def unit(x, carry):
        for h in every:
            root = field_ref[h, 1, x, chunk, :]
            inverse = jnp.where(root > 0.0, 1.0 / jnp.where(root > 0.0, root, 1.0), 0.0)
            heat = [va[c, h, x, chunk, :] * inverse for c in range(3)]
            size = jnp.sqrt(heat[0] * heat[0] + heat[1] * heat[1] + heat[2] * heat[2])
            scale = 0.5 / jnp.maximum(size, NORM_FLOOR)
            for c in range(3):
                vb[c, h, x, chunk, :] = heat[c] * scale
        return carry

    lax.fori_loop(STEPS, planes - STEPS, unit, 0)

    own_lane = lax.broadcasted_iota(jnp.int32, (own_y, LANES), 1)
    own_first, own_last = own_lane == 0, own_lane == LANES - 1
    block = out_ref.shape[2]
    batch = 2

    def transform(step, carry):
        one = jnp.minimum(step + 1, 1)
        slabs = []
        for j in range(batch * pack):
            x = HALO + step * (batch * pack) + j
            up, down = z_neighbours([vb[2, h, x, own_rows, :] for h in every], own_first, own_last)
            slabs.append(
                jnp.concatenate(
                    [
                        (vb[0, h, x + 1, own_rows, :] - vb[0, h, x - 1, own_rows, :])
                        + (
                            vb[1, h, x, pl.ds(PAD + one, own_y), :]
                            - vb[1, h, x, pl.ds(PAD - one, own_y), :]
                        )
                        + (up[h] - down[h])
                        for h in every
                    ],
                    axis=1,
                )
            )
        lines = halves(jnp.concatenate(slabs, axis=0))
        spectrum = product((cosine_ref[0], cosine_ref[1]), lines, NT)
        for q in range(batch):
            for g in range(groups):
                out_ref[g, step * batch + q] = spectrum[
                    g * block : (g + 1) * block, q * LANES : (q + 1) * LANES
                ]
        return carry

    lax.fori_loop(0, own_x // (pack * batch), transform, 0)


def lane_group_select(stacked, count, width):
    rows = stacked.shape[0] // count
    lane = lax.broadcasted_iota(jnp.int32, (rows, LANES), 1)
    chosen = stacked[:rows]
    for i in range(1, count):
        chosen = jnp.where(lane >= i * width, stacked[i * rows : (i + 1) * rows], chosen)
    return chosen


def rolled_stack(value, count, width):
    parts = [value] + [pltpu.roll(value, d * width, 1) for d in range(1, count)]
    return jnp.concatenate(parts, axis=0) if count > 1 else value


def forward_kernel(lines_ref, cx_ref, cy_ref, plane_ref, wave_z_ref, edge_ref, spec_ref, rim_ref, *, dims):
    block, pack, own_y, rows, batch = dims

    def some(step, carry):
        mixed = []
        for q in range(batch):
            lines = lines_ref[pl.ds(step * batch + q, rows, stride=block), :]
            stack = halves(rolled_stack(lines, pack, own_y))
            mixed.append(
                lane_group_select(product((cx_ref[0], cx_ref[1]), stack, NN), pack, own_y)
            )
        for q in range(batch):
            k = step * batch + q
            spec = product(halves(mixed[q]), (cy_ref[0], cy_ref[1]), NN)
            spec_ref[k] = spec
            local = spec / (plane_ref[...] + wave_z_ref[k, 0:1, :])
            ends = dot_nt(edge_ref[...], local)
            for e in range(2):
                for i in range(pack):
                    rim_ref[e, i, pl.ds(k, 1), :] = ends[e * pack + i : e * pack + i + 1]
        return carry

    lax.fori_loop(0, block // batch, some, 0)


def backward_kernel(
    place_ref, spec_ref, rims_ref, near_ref, far_ref, cx_ref, cy_ref, plane_ref, wave_z_ref, edge_ref,
    out_ref, push_ref, *, dims
):
    block, pack, own_y, rows, batch, parts = dims
    place = place_ref[0]
    for i in range(pack):
        near, far = near_ref[i], far_ref[i]
        diagonal = 1.0 + 2.0 * near
        jumps = [rims_ref[b, 1, i] - rims_ref[b + 1, 0, i] for b in range(parts - 1)]
        ratio, value = [], []
        for j in range(parts - 1):
            pivot = diagonal if j == 0 else diagonal - far * ratio[-1]
            inverse = 1.0 / pivot
            ratio.append(far * inverse)
            value.append((jumps[j] if j == 0 else jumps[j] + far * value[-1]) * inverse)
        for j in range(parts - 3, -1, -1):
            value[j] = value[j] + ratio[j] * value[j + 1]
        left = jnp.zeros_like(near)
        right = jnp.zeros_like(near)
        for j in range(parts - 1):
            left = jnp.where(place == j + 1, value[j], left)
            right = jnp.where(place == j, -value[j], right)
        push_ref[0, i] = left
        push_ref[1, i] = right

    fill = edge_ref.shape[0] - 2 * pack

    def some(step, carry):
        solved = []
        for q in range(batch):
            k = step * batch + q
            pushes = [push_ref[e, i, pl.ds(k, 1), :] for e in range(2) for i in range(pack)]
            if fill:
                pushes.append(jnp.zeros((fill, rows), jnp.float32))
            push = jnp.concatenate(pushes, axis=0)
            spec = spec_ref[k] + dot(push.T, edge_ref[...])
            solved.append(spec / (plane_ref[...] + wave_z_ref[k, 0:1, :]))
        for q in range(batch):
            lines = product(halves(solved[q]), (cy_ref[0], cy_ref[1]), NN)
            stack = halves(rolled_stack(lines, pack, own_y))
            mixed = product((cx_ref[0], cx_ref[1]), stack, NN)
            out_ref[pl.ds(step * batch + q, rows, stride=block), :] = lane_group_select(
                mixed, pack, own_y
            )
        return carry

    lax.fori_loop(0, block // batch, some, 0)


def last_kernel(lines_ref, cosine_ref, out_ref, *, dims):
    pack, own_y, tiles, batch = dims
    groups, packs, block, _ = lines_ref.shape

    def some(step, carry):
        for q in range(batch):
            xp = step * batch + q
            lines = jnp.concatenate([lines_ref[g, xp] for g in range(groups)], axis=0)
            values = product(halves(lines.T), (cosine_ref[0], cosine_ref[1]), NN)
            for j in range(pack):
                for h in range(tiles):
                    out_ref[h, xp * pack + j] = values[
                        j * own_y : (j + 1) * own_y, h * LANES : (h + 1) * LANES
                    ]
        return carry

    lax.fori_loop(0, packs // batch, some, 0)


def per_device(surface_ids, class_map, conductivity, normals, class_table):
    width_x, width_y, width_z = surface_ids.shape
    narrow, wide, outer = lax.axis_size("gz"), lax.axis_size("gy"), lax.axis_size("gx")
    length = width_z * narrow
    groups = outer * narrow
    own_x = width_x // narrow
    pack = LANES // width_y
    block = length // groups
    tiles = length // LANES
    rows = length // pack
    planes = own_x + 2 * HALO
    limit = 60 << 20

    class_value = jnp.zeros(class_map.shape, jnp.float32)
    for index in range(class_table.shape[0]):
        class_value = jnp.where(class_map == index, class_table[index], class_value)
    root = jnp.sqrt(class_value * conductivity)

    def split(values):
        values = values.reshape(narrow, own_x, width_y, width_z // LANES, LANES)
        return values.transpose(0, 3, 1, 2, 4)

    field = jnp.stack([split(surface_ids.astype(jnp.float32)), split(root)], axis=2)
    field = lax.all_to_all(field, "gz", split_axis=0, concat_axis=0, tiled=True)
    field = field.reshape(tiles, 2, own_x, width_y, LANES)

    axes = ("gx", "gy", "gz")

    def place(x, y):
        return (x // narrow * wide + y) * narrow + x % narrow

    def fetch(values, step_x, step_y):
        pairs = []
        for x in range(groups):
            for y in range(wide):
                if 0 <= x + step_x < groups and 0 <= y + step_y < wide:
                    pairs.append((place(x, y), place(x + step_x, y + step_y)))
        return lax.ppermute(values, axes, pairs)

    x_from = {1: slice(own_x - HALO, own_x), 0: slice(None), -1: slice(0, HALO)}
    y_from = {1: slice(width_y - HALO, width_y), 0: slice(None), -1: slice(0, HALO)}

    def beside(step_x, step_y):
        piece = field[:, :, x_from[step_x], y_from[step_y]]
        if step_y:
            piece = piece.reshape(tiles, 2, -1, LANES)
        return fetch(piece, step_x, step_y)

    pieces = [field] + [
        beside(*step)
        for step in ((1, 0), (-1, 0), (0, 1), (0, -1), (1, 1), (-1, 1), (1, -1), (-1, -1))
    ]
    extent = width_y + 2 * PAD

    entries = normals.shape[1]
    table_blocks = -(-entries // LANES)
    table = jnp.pad(normals, ((0, 0), (0, table_blocks * LANES - entries)))
    table = jnp.broadcast_to(
        table.reshape(3, table_blocks, 1, LANES), (3, table_blocks, SUBLANES, LANES)
    )
    cosine = cosine_table(length)
    lines = pl.pallas_call(
        functools.partial(
            diffuse_kernel, dims=(tiles, planes, extent, own_x, width_y, pack, groups)
        ),
        out_shape=jax.ShapeDtypeStruct((groups, own_x // pack, block, LANES), jnp.float32),
        in_specs=[pl.BlockSpec(memory_space=pl.ANY)] * 3
        + [pl.BlockSpec(memory_space=pltpu.VMEM)] * 8,
        scratch_shapes=[
            pltpu.VMEM((tiles, 2, planes, extent, LANES), jnp.float32),
            pltpu.VMEM((3, tiles, planes, extent, LANES), jnp.float32),
            pltpu.VMEM((3, tiles, planes, extent, LANES), jnp.float32),
            pltpu.VMEM((tiles, planes, extent, LANES), jnp.float32),
            pltpu.VMEM((tiles, planes, extent, LANES), jnp.float32),
            pltpu.VMEM((3, tiles, width_y + 2 * SUBLANES, LANES), jnp.float32),
            pltpu.VMEM((3, tiles, width_y + 2 * SUBLANES, LANES), jnp.float32),
            pltpu.SemaphoreType.DMA((3,)),
        ],
        compiler_params=pltpu.CompilerParams(vmem_limit_bytes=limit),
        name="diffuse",
    )(*pieces, table, table_halves(cosine))
    lines = lax.all_to_all(lines, ("gx", "gz"), split_axis=0, concat_axis=0, tiled=True)

    spectra = eigen_values(length)
    screen = np.float32(4.0 / (length * length))
    local = exact_table(width_y)
    local_values = 2.0 - 2.0 * np.cos(np.pi * np.arange(width_y) / width_y)
    order_x = np.arange(rows) // (own_x // pack) * own_x + np.arange(rows) % (own_x // pack) * pack
    forward_x = np.zeros((pack, rows, pack, rows), np.float32)
    inverse_x = np.zeros((pack, rows, pack, rows), np.float32)
    for i in range(pack):
        for d in range(pack):
            other = (i - d) % pack
            forward_x[i, :, d, :] = cosine[i * rows : (i + 1) * rows][:, order_x + other]
            inverse_x[i, :, d, :] = cosine[other * rows : (other + 1) * rows][:, order_x + i].T
    forward_x = forward_x.reshape(length, length)
    inverse_x = inverse_x.reshape(length, length)
    eye = np.eye(pack)
    forward_y = np.kron(eye, -local.T).astype(np.float32)
    inverse_y = np.kron(eye, local).astype(np.float32)
    edge = np.concatenate([np.kron(eye, local[:, 0][None]), np.kron(eye, local[:, -1][None])])
    edge_rows = -(-2 * pack // SUBLANES) * SUBLANES
    edge = np.pad(edge, ((0, edge_rows - 2 * pack), (0, 0))).astype(np.float32)
    spectra_x = spectra.reshape(pack, rows)
    plane = (
        spectra_x.T[:, :, None] + local_values.astype(np.float32)[None, None, :] + screen
    ).reshape(rows, LANES)
    shift = (spectra[:, None].astype(np.float64) + spectra[None, :] + float(screen))[:, :, None]
    weights = 1.0 / (shift + local_values)
    near = (weights @ (local[:, 0] ** 2)).astype(np.float32)
    far = (weights @ (local[:, 0] * local[:, -1])).astype(np.float32)
    near = near.reshape(length, pack, rows).transpose(1, 0, 2)
    far = far.reshape(length, pack, rows).transpose(1, 0, 2)
    group = lax.axis_index("gx") * narrow + lax.axis_index("gz")
    near, far = (
        lax.dynamic_slice_in_dim(jnp.asarray(t), group * block, block, axis=1) for t in (near, far)
    )
    wave_z = lax.dynamic_slice_in_dim(jnp.asarray(spectra), group * block, block)
    wave_z = jnp.broadcast_to(wave_z[:, None, None], (block, SUBLANES, LANES))
    plane, edge = jnp.asarray(plane), jnp.asarray(edge)

    spec, rim = pl.pallas_call(
        functools.partial(forward_kernel, dims=(block, pack, width_y, rows, 4)),
        out_shape=(
            jax.ShapeDtypeStruct((block, rows, LANES), jnp.float32),
            jax.ShapeDtypeStruct((2, pack, block, rows), jnp.float32),
        ),
        name="forward",
    )(
        lines.reshape(rows * block, LANES), table_halves(forward_x), table_halves(forward_y),
        plane, wave_z, edge,
    )
    rims = lax.all_gather(rim, "gy")
    solved = pl.pallas_call(
        functools.partial(backward_kernel, dims=(block, pack, width_y, rows, 4, wide)),
        out_shape=jax.ShapeDtypeStruct((rows * block, LANES), jnp.float32),
        in_specs=[pl.BlockSpec(memory_space=pltpu.SMEM)]
        + [pl.BlockSpec(memory_space=pltpu.VMEM)] * 9,
        scratch_shapes=[pltpu.VMEM((2, pack, block, rows), jnp.float32)],
        name="backward",
    )(
        lax.axis_index("gy").reshape(1).astype(jnp.int32), spec, rims, near, far,
        table_halves(inverse_x), table_halves(inverse_y), plane, wave_z, edge,
    )
    lines = solved.reshape(groups, own_x // pack, block, LANES)
    lines = lax.all_to_all(lines, ("gx", "gz"), split_axis=0, concat_axis=0, tiled=True)
    distance = pl.pallas_call(
        functools.partial(last_kernel, dims=(pack, width_y, tiles, 2)),
        out_shape=jax.ShapeDtypeStruct((tiles, own_x, width_y, LANES), jnp.float32),
        name="last",
    )(lines, table_halves(cosine))
    distance = distance.reshape(narrow, width_z // LANES, own_x, width_y, LANES)
    distance = lax.all_to_all(distance, "gz", split_axis=0, concat_axis=0, tiled=True)
    return distance.transpose(0, 2, 3, 1, 4).reshape(width_x, width_y, width_z)


def solution(mesh):
    in_specs = (P("gx", "gy", "gz"), P("gx", "gy", "gz"), P("gx", "gy", "gz"), P(), P())
    out_specs = P("gx", "gy", "gz")
    return jax.shard_map(
        per_device, mesh=mesh, in_specs=in_specs, out_specs=out_specs, check_vma=False
    )
```

time: 1510 us -> 294 us (0.19)
  local copies, waits for them, and re-layouts: 505 us -> 14.2 us
  other arithmetic: 344 us -> 6.14 us
  matrix products: 268 us -> 0 us
  starting transfers between devices: 188 us -> 26 us
  Pallas kernels: 0 us -> 136 us
  waiting for transfers between devices: 129 us -> 49.7 us
    dot_general x70 -> x0, matrix products: 268 us -> none  [the longest x64 223 us: one_block(): jnp.einsum('ck,nk->cn', lookup_table, one_hot, precision=lax.Precision.HI...]
    add x13 -> x0, other arithmetic: 237 us -> none  [the longest x8 229 us: diffuse(): return center + time_step * middle * inflow]
    slice x43 -> x10, local copies, waits for them, and re-layouts: 201 us -> 4.43 us  [the longest x9 2.96 us: beside(): piece = field[:, :, x_from[step_x], y_from[step_y]]]
    ppermute x60 -> x8, starting transfers between devices: 174 us -> 18.2 us  [fetch(): return lax.ppermute(values, axes, pairs)]
    pallas_call x0 -> x4, Pallas kernels: none -> 136 us  [the longest x1 98 us: per_device(): pl.pallas_call(functools.partial(diffuse_kernel, dims=(tiles, planes, ext...]
    ppermute x22 -> x0, local copies, waits for them, and re-layouts: 84 us -> none  [the longest x11 42.3 us: padded_2(): lax.ppermute(tail, axis, [(i, (i + 1) % count) for i in range(ends)])]
    all_to_all x3 -> x1, waiting for transfers between devices: 99.5 us -> 25.1 us  [per_device(): lax.all_to_all(lines, ('gx', 'gz'), split_axis=0, concat_axis=0, tiled=True)]
    reshape x14 -> x6, local copies, waits for them, and re-layouts: 74.9 us -> 2.51 us  [beside(): piece = piece.reshape(tiles, 2, -1, LANES)]
  transfers between devices with their start and end apart: 63 -> 9, of which waited for: 31 -> 2; matrix products, arithmetic and copies ran while one was open for 31% -> 2% of each run, Pallas kernels for 0% -> 0%
where the time goes in v1:
time: 294 us; the launch traced here: 293 us
  Pallas kernels  136 us (46%)
  blocking collectives  60.2 us (20%)
  waiting for transfers between devices  49.7 us (17%)
  starting transfers between devices  26 us (9%)
  local copies, waits for them, and re-layouts  14.2 us (5%)
  other arithmetic  6.14 us (2%)
    pallas_call x1, Pallas kernels, per_device(): pl.pallas_call(functools.partial(diffuse_kernel, dims=(tiles, planes, ext...  98 us
    all_to_all x1, blocking collectives, per_device(): lax.all_to_all(lines, ('gx', 'gz'), split_axis=0, concat_axis=0, tiled=True)  30.9 us
    all_to_all x1, waiting for transfers between devices, per_device(): lax.all_to_all(lines, ('gx', 'gz'), split_axis=0, concat_axis=0, tiled=True)  25.1 us
    ppermute x8, waiting for transfers between devices, fetch(): return lax.ppermute(values, axes, pairs)  24.5 us
    pallas_call x1, Pallas kernels, per_device(): pl.pallas_call(functools.partial(backward_kernel, dims=(block, pack, widt...  18.3 us
    ppermute x8, starting transfers between devices, fetch(): return lax.ppermute(values, axes, pairs)  18.2 us
    all_gather x1, blocking collectives, per_device(): rims = lax.all_gather(rim, 'gy')  15.5 us
    pallas_call x1, Pallas kernels, per_device(): pl.pallas_call(functools.partial(forward_kernel, dims=(block, pack, width...  14.3 us
  transfers between devices with their start and end apart: 9, of which 2 were waited for; matrix products, arithmetic and copies ran while one was open for 2% of the time, Pallas kernels for 0%

profile of v1, /device:TPU:0, one launch (start us, length us, event | category | flops | bytes accessed | tf_op | source)
XLA Modules:
  0.0 292.8 jit_solution(11059374897567878421)
XLA Ops:
  0.0 1.5 fusion.3
  1.5 1.9 convert_element_type.3
  3.4 0.3 copy-done.2
  3.7 0.6 copy-done.3
  4.3 3.7 %multiply_sqrt_fusion = f32[64,64,128]{2,1,0:T(8,128)S(1)} fusion(f32[64,64,128]{2,1,0:T(8,128)S(1)} %copy-done.2, s32[64,64,128]{2,1,0:T(8,128)S(1)} %copy-done.3, f32[]{:T(128)} %bitcast.5, f32[]{:T(128)} %bitcast.4, f32[]{:T(128)} %bitcast.3, f32[]{:T(128)} %bitcast.2), kind=kLoop, calls=%fused_computation.1 | loop fusion | flops 4718592 | bytes 6291472 | tf_op jit(solution)/shard_map/sqrt | solution.py:408
  8.0 0.6 pad_maximum_fusion
  8.6 7.1 %all_to_all.20 = f32[2,1,2,32,64,128]{5,4,3,2,1,0:T(8,128)S(1)} all-to-all(f32[2,1,2,32,64,128]{5,4,3,2,1,0:T(8,128)S(1)} %pad_maximum_fusion), channel_id=1, replica_groups=mesh['gx'=4,'gy'=4,'gz'=2] {'gz'}, dimensions={0} | all-to-all | bytes 8388608 | tf_op jit(solution)/shard_map/all_to_all | solution.py:415
  15.7 1.4 fusion.2
  17.1 2.1 collective-permute-start
  19.2 1.3 collective-permute-start.1
  20.5 0.1 fusion
  20.6 0.1 copy.33
  20.7 6.6 %collective-permute-start.4 = (f32[2,2,81,128]{3,2,1,0:T(8,128)S(1)}, f32[2,2,81,128]{3,2,1,0:T(8,128)S(1)}, u32[]{:S(2)}, u32[]{:S(2)}) collective-permute-start(f32[2,2,81,128]{3,2,1,0:T(8,128)S(1)} %copy.34), channel_id=1, source_target_pairs={{0,3},{2,5},{4,7},{1,10},{3,12},{5,14},{8,11},{10,13},{12,15},{9,1... | collective-permute-start | bytes 497672 | tf_op jit(solution)/shard_map/ppermute | solution.py:429
  27.3 0.2 fusion.1
  27.5 0.5 copy.29
  28.0 0.9 copy.30
  28.9 4.3 %collective-permute-start.2 = (f32[2,2,288,128]{3,2,1,0:T(8,128)}, f32[2,2,288,128]{3,2,1,0:T(8,128)}, u32[]{:S(2)}, u32[]{:S(2)}) collective-permute-start(f32[2,2,288,128]{3,2,1,0:T(8,128)} %copy.30), channel_id=1, source_target_pairs={{0,2},{2,4},{4,6},{1,3},{3,5},{5,7},{8,10},{10,12},{12,14},{9,11},... | collective-permute-start | bytes 1769480 | tf_op jit(solution)/shard_map/ppermute | solution.py:429
  33.2 0.5 copy.31
  33.6 0.0 copy-start.9
  33.7 0.9 copy.32
  34.5 1.3 collective-permute-start.3
  35.8 0.1 copy.35
  36.0 0.7 collective-permute-start.5
  36.6 0.1 copy.37
  36.8 0.7 collective-permute-start.6
  37.5 0.1 copy.39
  37.6 0.7 copy.40
  38.3 0.7 copy-done.8
  39.0 1.3 collective-permute-start.7
  40.3 24.5 %collective-permute-done.7.ne_ref = f32[2,2,81,128]{3,2,1,0:T(8,128)} collective-permute-done((f32[2,2,81,128]{3,2,1,0:T(8,128)}, f32[2,2,81,128]{3,2,1,0:T(8,128)}, u32[]{:S(2)}, u32[]{:S(2)}) %collective-permute-start.7) | collective-permute-done | bytes 165920 | tf_op jit(solution)/shard_map/ppermute | solution.py:429
  64.8 0.7 broadcast_in_dim.35.table_ref
  65.5 0.4 copy-done.4
  65.9 0.3 copy-done.5
  66.3 98.0 %diffuse.1 = f32[8,16,32,128]{3,2,1,0:T(8,128)} custom-call(f32[2,2,32,64,128]{4,3,2,1,0:T(8,128)} %bitcast.24, f32[2,2,9,64,128]{4,3,2,1,0:T(8,128)} %copy-done.4, f32[2,2,9,64,128]{4,3,2,1,0:T(8,128)} %copy-done.5, f32[2,2,288,128]{3,2,1,0:T(8,128)} %collective-permute-done.2.south_ref, f32[2,2,288,128]{3,2,1,0:T(8,128)} %collective-permute-done.3.north_ref, ...), custom_call_target="tpu_custom_call" | custom-call | tf_op jit(solution)/shard_map/diffuse/pallas_call | solution.py:453
  164.3 0.0 copy-start.10
  164.3 7.8 %all-to-all-start.1 = ((f32[8,16,32,128]{3,2,1,0:T(8,128)}), f32[8,16,32,128]{3,2,1,0:T(8,128)S(1)}, u32[]{:S(2)}, u32[]{:S(2)}) async-start(f32[8,16,32,128]{3,2,1,0:T(8,128)} %diffuse.1), calls=%async_computation.1 | async-start | bytes 4194304 | tf_op jit(solution)/shard_map/all_to_all | solution.py:473
  172.1 0.1 dynamic_slice.9
  172.2 1.4 constant_dynamic-slice_fusion
  173.6 25.1 %all-to-all-done.1 = f32[8,16,32,128]{3,2,1,0:T(8,128)S(1)} async-done(((f32[8,16,32,128]{3,2,1,0:T(8,128)}), f32[8,16,32,128]{3,2,1,0:T(8,128)S(1)}, u32[]{:S(2)}, u32[]{:S(2)}) %all-to-all-start.1) | async-done | bytes 2097184 | tf_op jit(solution)/shard_map/all_to_all | solution.py:473
  198.7 1.0 broadcast_in_dim.36.wave_z_ref
  199.6 0.4 copy-done.1
  200.0 14.3 %forward.1 = (f32[32,128,128]{2,1,0:T(8,128)}, f32[2,2,32,128]{3,2,1,0:T(8,128)}) custom-call(f32[4096,128]{1,0:T(8,128)} %bitcast.25, bf16[2,256,256]{2,1,0:T(8,128)(2,1)} %constant.53.clone.cx_ref, bf16[2,128,128]{2,1,0:T(8,128)(2,1)} %constant.54.clone.cy_ref, f32[128,128]{1,0:T(8,128)} %constant.51.clone.plane_ref, ...), custom_call_target="tpu_custom_call" | custom-call | tf_op jit(solution)/shard_map/forward/pallas_call | solution.py:513
  214.4 15.5 %all-gather = f32[8,2,32,128]{3,2,1,0:T(8,128)} all-gather(f32[2,2,32,128]{3,2,1,0:T(8,128)} %get-tuple-element.8), channel_id=2, replica_groups=mesh['gx'=4,'gy'=4,'gz'=2] {'gy'}, dimensions={0}, use_global_device_ids=true | all-gather | bytes 327680 | tf_op jit(solution)/shard_map/all_gather | solution.py:524
  229.9 18.3 %backward.1 = f32[4096,128]{1,0:T(8,128)} custom-call(s32[1]{0:T(128)} %bitcast.place_ref, f32[32,128,128]{2,1,0:T(8,128)} %get-tuple-element.7.spec_ref, f32[4,2,2,32,128]{4,3,2,1,0:T(8,128)} %bitcast.33, f32[2,32,128]{2,1,0:T(8,128)} %get-tuple-element.22.near_ref, f32[2,32,128]{2,1,0:T(8,128)} %get-tuple-element.21.far_ref, ...), custom_call_target="tpu_custom_call" | custom-call | tf_op jit(solution)/shard_map/backward/pallas_call | solution.py:525
  248.3 30.9 %all_to_all.21.lines_ref = f32[8,16,32,128]{3,2,1,0:T(8,128)} all-to-all(f32[8,16,32,128]{3,2,1,0:T(8,128)} %bitcast.26), channel_id=1, replica_groups=mesh['gx'=4,'gy'=4,'gz'=2] {'gx','gz'}, dimensions={0} | all-to-all | bytes 4194304 | tf_op jit(solution)/shard_map/all_to_all | solution.py:537
  279.2 5.7 %last.1 = f32[2,32,64,128]{3,2,1,0:T(8,128)} custom-call(f32[8,16,32,128]{3,2,1,0:T(8,128)} %all_to_all.21.lines_ref, bf16[2,256,256]{2,1,0:T(8,128)(2,1)} %constant.47.clone.cosine_ref), custom_call_target="tpu_custom_call" | custom-call | tf_op jit(solution)/shard_map/last/pallas_call | solution.py:538
  284.9 6.6 %all_to_all.22 = f32[2,1,32,64,128]{4,3,2,1,0:T(8,128)S(1)} all-to-all(f32[2,1,32,64,128]{4,3,2,1,0:T(8,128)} %bitcast.27), channel_id=1, replica_groups=mesh['gx'=4,'gy'=4,'gz'=2] {'gz'}, dimensions={0} | all-to-all | bytes 4194304 | tf_op jit(solution)/shard_map/all_to_all | solution.py:544
  291.5 1.3 copy.43
  (25 shorter events, 0.1 us)
Async XLA Ops:
  1.5 2.2 copy-start.2
  1.5 2.9 copy-start.3
  15.7 11.7 %copy-start = (f32[2,1,2,32,64,128]{5,4,3,2,1,0:T(8,128)}, f32[2,1,2,32,64,128]{5,4,3,2,1,0:T(8,128)S(1)}, u32[]{:S(2)}) copy-start(f32[2,1,2,32,64,128]{5,4,3,2,1,0:T(8,128)S(1)} %all_to_all.20) | copy-start | bytes 12582916
  17.1 47.7 %collective-permute-start = (f32[2,2,9,64,128]{4,3,2,1,0:T(8,128)}, f32[2,2,9,64,128]{4,3,2,1,0:T(8,128)S(1)}, u32[]{:S(2)}, u32[]{:S(2)}) collective-permute-start(f32[2,2,9,64,128]{4,3,2,1,0:T(8,128)} %get-tuple-element.16), channel_id=1, source_target_pairs={{0,1},{2,3},{4,5},{6,7},{1,8},{3,10},{5,12},{7,14},{8,9},{10,11},{... | collective-permute-start | bytes 3538952 | tf_op jit(solution)/shard_map/ppermute | solution.py:429
  19.2 45.6 %collective-permute-start.1 = (f32[2,2,9,64,128]{4,3,2,1,0:T(8,128)S(1)}, f32[2,2,9,64,128]{4,3,2,1,0:T(8,128)S(1)}, u32[]{:S(2)}, u32[]{:S(2)}) collective-permute-start(f32[2,2,9,64,128]{4,3,2,1,0:T(8,128)S(1)} %get-tuple-element.15), channel_id=1, source_target_pairs={{1,0},{3,2},{5,4},{7,6},{8,1},{10,3},{12,5},{14,7},{9,8},{11,10},{... | collective-permute-start | bytes 3538952 | tf_op jit(solution)/shard_map/ppermute | solution.py:429
  20.7 15.2 %collective-permute-start.4 = (f32[2,2,81,128]{3,2,1,0:T(8,128)S(1)}, f32[2,2,81,128]{3,2,1,0:T(8,128)S(1)}, u32[]{:S(2)}, u32[]{:S(2)}) collective-permute-start(f32[2,2,81,128]{3,2,1,0:T(8,128)S(1)} %copy.34), channel_id=1, source_target_pairs={{0,3},{2,5},{4,7},{1,10},{3,12},{5,14},{8,11},{10,13},{12,15},{9,1... | collective-permute-start | bytes 497672 | tf_op jit(solution)/shard_map/ppermute | solution.py:429
  28.9 35.9 %collective-permute-start.2 = (f32[2,2,288,128]{3,2,1,0:T(8,128)}, f32[2,2,288,128]{3,2,1,0:T(8,128)}, u32[]{:S(2)}, u32[]{:S(2)}) collective-permute-start(f32[2,2,288,128]{3,2,1,0:T(8,128)} %copy.30), channel_id=1, source_target_pairs={{0,2},{2,4},{4,6},{1,3},{3,5},{5,7},{8,10},{10,12},{12,14},{9,11},... | collective-permute-start | bytes 1769480 | tf_op jit(solution)/shard_map/ppermute | solution.py:429
  33.6 6.6 %copy-start.9 = (f32[3,256]{1,0:T(4,128)S(1)}, f32[3,256]{1,0:T(4,128)}, u32[]{:S(2)}) copy-start(f32[3,256]{1,0:T(4,128)} %param.19) | copy-start | bytes 9220
  34.5 30.3 %collective-permute-start.3 = (f32[2,2,288,128]{3,2,1,0:T(8,128)}, f32[2,2,288,128]{3,2,1,0:T(8,128)}, u32[]{:S(2)}, u32[]{:S(2)}) collective-permute-start(f32[2,2,288,128]{3,2,1,0:T(8,128)} %copy.32), channel_id=1, source_target_pairs={{2,0},{4,2},{6,4},{3,1},{5,3},{7,5},{10,8},{12,10},{14,12},{11,9},... | collective-permute-start | bytes 1769480 | tf_op jit(solution)/shard_map/ppermute | solution.py:429
  36.0 2.3 copy-start.6
  36.0 0.8 collective-permute-start.5
  36.8 1.5 copy-start.7
  36.8 1.5 collective-permute-start.6
  38.3 0.7 copy-start.8
  39.0 25.8 %collective-permute-start.7 = (f32[2,2,81,128]{3,2,1,0:T(8,128)}, f32[2,2,81,128]{3,2,1,0:T(8,128)}, u32[]{:S(2)}, u32[]{:S(2)}) collective-permute-start(f32[2,2,81,128]{3,2,1,0:T(8,128)} %copy.40), channel_id=1, source_target_pairs={{3,0},{5,2},{7,4},{10,1},{12,3},{14,5},{11,8},{13,10},{15,12},{18,... | collective-permute-start | bytes 497672 | tf_op jit(solution)/shard_map/ppermute | solution.py:429
  64.8 1.1 copy-start.4
  64.8 1.4 copy-start.5
  164.3 7.8 %copy-start.10 = (f32[256]{0:T(256)S(1)}, f32[256]{0:T(256)}, u32[]{:S(2)}) copy-start(f32[256]{0:T(256)} %constant.50.clone) | copy-start | bytes 3076
  164.3 34.4 %all-to-all-start.1 = ((f32[8,16,32,128]{3,2,1,0:T(8,128)}), f32[8,16,32,128]{3,2,1,0:T(8,128)S(1)}, u32[]{:S(2)}, u32[]{:S(2)}) async-start(f32[8,16,32,128]{3,2,1,0:T(8,128)} %diffuse.1), calls=%async_computation.1 | async-start | bytes 4194304 | tf_op jit(solution)/shard_map/all_to_all | solution.py:473
  198.7 1.4 copy-start.1

commit v2 on v1

--- a/solution.py
+++ b/solution.py
@@ -74,16 +74,13 @@
 
 
 def z_neighbours(tiles, first, last):
-    below = [pltpu.roll(t, 1, 1) for t in tiles]
-    above = [pltpu.roll(t, LANES - 1, 1) for t in tiles]
-    count = len(tiles)
-    down = [jnp.where(first, below[h - 1] if h else 0.0, below[h]) for h in range(count)]
-    up = [jnp.where(last, above[h + 1] if h + 1 < count else 0.0, above[h]) for h in range(count)]
-    return up, down
+    above = jnp.where(last, 0.0, pltpu.roll(tiles[0], LANES - 1, 1))
+    below = jnp.where(first, 0.0, pltpu.roll(tiles[-1], 1, 1))
+    return [*tiles[1:], above], [below, *tiles[:-1]]
 
 
 def diffuse_kernel(
-    own_ref, west_ref, east_ref, south_ref, north_ref, sw_ref, se_ref, nw_ref, ne_ref, table_ref, cosine_ref,
+    own_ref, west_ref, east_ref, south_ref, north_ref, sw_ref, se_ref, nw_ref, ne_ref, table_ref, order_ref, cosine_ref,
     out_ref, field_ref, va, vb, keep_ref, gain_ref, za, zb, sems, *, dims
 ):
     tiles, planes, rows, own_x, own_y, pack, groups = dims
@@ -133,15 +130,32 @@
     for copy in copies:
         copy.wait()
 
+    used = pl.ds(0, span + 2 * SUBLANES)
+
+    def reorder(x, carry):
+        for f, parts in ((0, 1 if table_blocks * LANES <= 256 else 2), (1, 3)):
+            rest = jnp.concatenate([field_ref[h, f, x, used, :] for h in every], axis=1)
+            moved = None
+            for _ in range(parts):
+                part = rest.astype(jnp.bfloat16)
+                rest = rest - part.astype(jnp.float32)
+                picked = jnp.dot(part, order_ref[...], preferred_element_type=jnp.float32)
+                moved = picked if moved is None else moved + picked
+            for h in every:
+                field_ref[h, f, x, used, :] = moved[:, h * LANES : (h + 1) * LANES]
+        return carry
+
+    lax.fori_loop(0, planes, reorder, 0)
+
     row = lax.broadcasted_iota(jnp.int32, (SUBLANES, LANES), 0)
 
     def spread(x):
-        for y in range(rows // SUBLANES):
+        for y in range(span // SUBLANES + 2):
             at = pl.ds(y * SUBLANES, SUBLANES)
             for h in every:
                 ids = field_ref[h, 0, x, at, :]
                 root = field_ref[h, 1, x, at, :]
-                if y == 0 or y == rows // SUBLANES - 1:
+                if y == 0 or y == span // SUBLANES + 1:
                     inside = row == (SUBLANES - 1 if y == 0 else 0)
                     ids = jnp.where(inside, ids, 0.0)
                     root = jnp.where(inside, root, 0.0)
@@ -191,35 +205,38 @@
             for h in every:
                 kept[c, h, pl.ds(y * SUBLANES, SUBLANES), :] = up[h] + down[h]
 
-    def update(source, target, x, y, kept, one):
+    def update(source, target, x, y, one):
         base = SUBLANES * (y + 1)
         at = pl.ds(base, SUBLANES)
         for h in every:
-            keep, gain = keep_ref[h, x, at, :], gain_ref[h, x, at, :]
+            keep = [keep_ref[h, x + i, at, :] for i in range(2)]
+            gain = [gain_ref[h, x + i, at, :] for i in range(2)]
             for c in range(3):
-                total = (
-                    (source[c, h, x + 1, at, :] + source[c, h, x - 1, at, :])
-                    + (
-                        source[c, h, x, pl.ds(base + one, SUBLANES), :]
-                        + source[c, h, x, pl.ds(base - one, SUBLANES), :]
+                line = [source[c, h, x + i, at, :] for i in range(-1, 3)]
+                for i, kept in enumerate((za, zb)):
+                    total = (
+                        (line[i] + line[i + 2])
+                        + (
+                            source[c, h, x + i, pl.ds(base + one, SUBLANES), :]
+                            + source[c, h, x + i, pl.ds(base - one, SUBLANES), :]
+                        )
+                        + kept[c, h, pl.ds(y * SUBLANES, SUBLANES), :]
                     )
-                    + kept[c, h, pl.ds(y * SUBLANES, SUBLANES), :]
-                )
-                target[c, h, x, at, :] = keep * source[c, h, x, at, :] + gain * total
+                    target[c, h, x + i, at, :] = keep[i] * line[i + 1] + gain[i] * total
 
     def sweep(source, target, begin):
         for y in range(span // SUBLANES):
             along_z(source, begin, y, za)
+            along_z(source, begin + 1, y, zb)
 
         def two_planes(pair, carry):
             x = begin + 2 * pair
             one = jnp.minimum(x, 1)
+            ahead = jnp.minimum(x + 3, planes - 1)
             for y in range(span // SUBLANES):
-                update(source, target, x, y, za, one)
-                along_z(source, x + 1, y, zb)
-            for y in range(span // SUBLANES):
-                update(source, target, x + 1, y, zb, one)
+                update(source, target, x, y, one)
                 along_z(source, x + 2, y, za)
+                along_z(source, ahead, y, zb)
             return carry
 
         lax.fori_loop(0, planes // 2 - begin, two_planes, 0)
@@ -329,7 +346,8 @@
     for i in range(pack):
         near, far = near_ref[i], far_ref[i]
         diagonal = 1.0 + 2.0 * near
-        jumps = [rims_ref[b, 1, i] - rims_ref[b + 1, 0, i] for b in range(parts - 1)]
+        at = [(place + (parts - b)) % parts for b in range(parts)]
+        jumps = [rims_ref[at[b], 1, i] - rims_ref[at[b + 1], 0, i] for b in range(parts - 1)]
         ratio, value = [], []
         for j in range(parts - 1):
             pivot = diagonal if j == 0 else diagonal - far * ratio[-1]
@@ -441,7 +459,7 @@
         beside(*step)
         for step in ((1, 0), (-1, 0), (0, 1), (0, -1), (1, 1), (-1, 1), (1, -1), (-1, -1))
     ]
-    extent = width_y + 2 * PAD
+    extent = width_y + 2 * PAD + SUBLANES
 
     entries = normals.shape[1]
     table_blocks = -(-entries // LANES)
@@ -450,13 +468,15 @@
         table.reshape(3, table_blocks, 1, LANES), (3, table_blocks, SUBLANES, LANES)
     )
     cosine = cosine_table(length)
+    cells = np.arange(length) % LANES * tiles + np.arange(length) // LANES
+    order = np.arange(length)[:, None] == cells[None, :]
     lines = pl.pallas_call(
         functools.partial(
             diffuse_kernel, dims=(tiles, planes, extent, own_x, width_y, pack, groups)
         ),
         out_shape=jax.ShapeDtypeStruct((groups, own_x // pack, block, LANES), jnp.float32),
         in_specs=[pl.BlockSpec(memory_space=pl.ANY)] * 3
-        + [pl.BlockSpec(memory_space=pltpu.VMEM)] * 8,
+        + [pl.BlockSpec(memory_space=pltpu.VMEM)] * 9,
         scratch_shapes=[
             pltpu.VMEM((tiles, 2, planes, extent, LANES), jnp.float32),
             pltpu.VMEM((3, tiles, planes, extent, LANES), jnp.float32),
@@ -469,7 +489,7 @@
         ],
         compiler_params=pltpu.CompilerParams(vmem_limit_bytes=limit),
         name="diffuse",
-    )(*pieces, table, table_halves(cosine))
+    )(*pieces, table, jnp.asarray(order.astype(jnp.bfloat16)), table_halves(cosine[:, cells]))
     lines = lax.all_to_all(lines, ("gx", "gz"), split_axis=0, concat_axis=0, tiled=True)
 
     spectra = eigen_values(length)
@@ -521,7 +541,13 @@
         lines.reshape(rows * block, LANES), table_halves(forward_x), table_halves(forward_y),
         plane, wave_z, edge,
     )
-    rims = lax.all_gather(rim, "gy")
+    rims = jnp.stack(
+        [rim]
+        + [
+            lax.ppermute(rim, "gy", [(i, (i + step) % wide) for i in range(wide)])
+            for step in range(1, wide)
+        ]
+    )
     solved = pl.pallas_call(
         functools.partial(backward_kernel, dims=(block, pack, width_y, rows, 4, wide)),
         out_shape=jax.ShapeDtypeStruct((rows * block, LANES), jnp.float32),

time: 294 us -> 281 us (0.956)
  blocking collectives: 60.2 us -> 44.6 us
  Pallas kernels: 136 us -> 129 us
  starting transfers between devices: 26 us -> 31.8 us
  waiting for transfers between devices: 49.7 us -> 52.8 us
    all_gather x1 -> x0, blocking collectives: 15.5 us -> none  [per_device(): rims = lax.all_gather(rim, 'gy')]
    pallas_call x1, Pallas kernels: 98 us -> 90.6 us  [per_device(): pl.pallas_call(functools.partial(diffuse_kernel, dims=(tiles, planes, ext...]
    ppermute x0 -> x3, starting transfers between devices: none -> 5.86 us  [per_device(): lax.ppermute(rim, 'gy', [(i, (i + step) % wide) for i in range(wide)])]
  transfers between devices with their start and end apart: 9 -> 12, of which waited for: 2 -> 3; matrix products, arithmetic and copies ran while one was open for 2% -> 2% of each run, Pallas kernels for 0% -> 0%
where the time goes in v2:
time: 281 us; the launch traced here: 280 us
  Pallas kernels  129 us (46%)
  waiting for transfers between devices  52.8 us (19%)
  blocking collectives  44.6 us (16%)
  starting transfers between devices  31.8 us (11%)
  local copies, waits for them, and re-layouts  14.1 us (5%)
  other arithmetic  7.69 us (3%)
    pallas_call x1, Pallas kernels, per_device(): pl.pallas_call(functools.partial(diffuse_kernel, dims=(tiles, planes, ext...  90.6 us
    all_to_all x1, blocking collectives, per_device(): lax.all_to_all(lines, ('gx', 'gz'), split_axis=0, concat_axis=0, tiled=True)  30.9 us
    all_to_all x1, waiting for transfers between devices, per_device(): lax.all_to_all(lines, ('gx', 'gz'), split_axis=0, concat_axis=0, tiled=True)  26.5 us
    ppermute x8, waiting for transfers between devices, fetch(): return lax.ppermute(values, axes, pairs)  24.6 us
    pallas_call x1, Pallas kernels, per_device(): pl.pallas_call(functools.partial(backward_kernel, dims=(block, pack, widt...  18.3 us
    ppermute x8, starting transfers between devices, fetch(): return lax.ppermute(values, axes, pairs)  18.2 us
    pallas_call x1, Pallas kernels, per_device(): pl.pallas_call(functools.partial(forward_kernel, dims=(block, pack, width...  14.3 us
    all_to_all x1, starting transfers between devices, per_device(): lax.all_to_all(lines, ('gx', 'gz'), split_axis=0, concat_axis=0, tiled=True)  7.79 us
  transfers between devices with their start and end apart: 12, of which 3 were waited for; matrix products, arithmetic and copies ran while one was open for 2% of the time, Pallas kernels for 0%

profile of v2, /device:TPU:0, one launch (start us, length us, event | category | flops | bytes accessed | tf_op | source)
XLA Modules:
  0.0 280.3 jit_solution(5754338764511820498)
XLA Ops:
  0.0 1.5 fusion.3
  1.5 1.9 convert_element_type.3
  3.4 0.3 copy-done.2
  3.7 0.6 copy-done.3
  4.3 3.7 %multiply_sqrt_fusion = f32[64,64,128]{2,1,0:T(8,128)S(1)} fusion(f32[64,64,128]{2,1,0:T(8,128)S(1)} %copy-done.2, s32[64,64,128]{2,1,0:T(8,128)S(1)} %copy-done.3, f32[]{:T(128)} %bitcast.5, f32[]{:T(128)} %bitcast.4, f32[]{:T(128)} %bitcast.3, f32[]{:T(128)} %bitcast.2), kind=kLoop, calls=%fused_computation.1 | loop fusion | flops 4718592 | bytes 6291472 | tf_op jit(solution)/shard_map/sqrt | solution.py:426
  8.0 0.6 pad_maximum_fusion
  8.6 7.1 %all_to_all.20 = f32[2,1,2,32,64,128]{5,4,3,2,1,0:T(8,128)S(1)} all-to-all(f32[2,1,2,32,64,128]{5,4,3,2,1,0:T(8,128)S(1)} %pad_maximum_fusion), channel_id=1, replica_groups=mesh['gx'=4,'gy'=4,'gz'=2] {'gz'}, dimensions={0} | all-to-all | bytes 8388608 | tf_op jit(solution)/shard_map/all_to_all | solution.py:433
  15.7 1.4 fusion.2
  17.1 2.1 collective-permute-start
  19.2 1.3 collective-permute-start.1
  20.5 0.1 fusion
  20.6 0.1 copy.34
  20.7 6.6 %collective-permute-start.4 = (f32[2,2,81,128]{3,2,1,0:T(8,128)S(1)}, f32[2,2,81,128]{3,2,1,0:T(8,128)S(1)}, u32[]{:S(2)}, u32[]{:S(2)}) collective-permute-start(f32[2,2,81,128]{3,2,1,0:T(8,128)S(1)} %copy.35), channel_id=1, source_target_pairs={{0,3},{2,5},{4,7},{1,10},{3,12},{5,14},{8,11},{10,13},{12,15},{9,1... | collective-permute-start | bytes 497672 | tf_op jit(solution)/shard_map/ppermute | solution.py:447
  27.4 0.2 fusion.1
  27.6 0.5 copy.30
  28.0 0.9 copy.31
  28.9 4.3 %collective-permute-start.2 = (f32[2,2,288,128]{3,2,1,0:T(8,128)}, f32[2,2,288,128]{3,2,1,0:T(8,128)}, u32[]{:S(2)}, u32[]{:S(2)}) collective-permute-start(f32[2,2,288,128]{3,2,1,0:T(8,128)} %copy.31), channel_id=1, source_target_pairs={{0,2},{2,4},{4,6},{1,3},{3,5},{5,7},{8,10},{10,12},{12,14},{9,11},... | collective-permute-start | bytes 1769480 | tf_op jit(solution)/shard_map/ppermute | solution.py:447
  33.2 0.5 copy.32
  33.6 0.9 copy.33
  34.5 1.3 collective-permute-start.3
  35.8 0.1 copy.36
  35.9 0.7 collective-permute-start.5
  36.7 0.7 collective-permute-start.6
  37.4 0.1 copy.40
  37.5 0.7 copy.41
  38.2 0.7 copy-done.8
  38.9 1.3 collective-permute-start.7
  40.2 24.6 %collective-permute-done.7.ne_ref = f32[2,2,81,128]{3,2,1,0:T(8,128)} collective-permute-done((f32[2,2,81,128]{3,2,1,0:T(8,128)}, f32[2,2,81,128]{3,2,1,0:T(8,128)}, u32[]{:S(2)}, u32[]{:S(2)}) %collective-permute-start.7) | collective-permute-done | bytes 165920 | tf_op jit(solution)/shard_map/ppermute | solution.py:447
  64.8 0.7 broadcast_in_dim.35.table_ref
  65.5 0.4 copy-done.4
  65.8 0.4 copy-done.5
  66.2 90.6 %diffuse.1 = f32[8,16,32,128]{3,2,1,0:T(8,128)} custom-call(f32[2,2,32,64,128]{4,3,2,1,0:T(8,128)} %bitcast.27, f32[2,2,9,64,128]{4,3,2,1,0:T(8,128)} %copy-done.4, f32[2,2,9,64,128]{4,3,2,1,0:T(8,128)} %copy-done.5, f32[2,2,288,128]{3,2,1,0:T(8,128)} %collective-permute-done.2.south_ref, f32[2,2,288,128]{3,2,1,0:T(8,128)} %collective-permute-done.3.north_ref, ...), custom_call_target="tpu_custom_call" | custom-call | tf_op jit(solution)/shard_map/diffuse/pallas_call | solution.py:473
  156.9 7.8 %all-to-all-start.1 = ((f32[8,16,32,128]{3,2,1,0:T(8,128)}), f32[8,16,32,128]{3,2,1,0:T(8,128)S(1)}, u32[]{:S(2)}, u32[]{:S(2)}) async-start(f32[8,16,32,128]{3,2,1,0:T(8,128)} %diffuse.1), calls=%async_computation.1 | async-start | bytes 4194304 | tf_op jit(solution)/shard_map/all_to_all | solution.py:493
  164.7 26.5 %all-to-all-done.1 = f32[8,16,32,128]{3,2,1,0:T(8,128)S(1)} async-done(((f32[8,16,32,128]{3,2,1,0:T(8,128)}), f32[8,16,32,128]{3,2,1,0:T(8,128)S(1)}, u32[]{:S(2)}, u32[]{:S(2)}) %all-to-all-start.1) | async-done | bytes 2097184 | tf_op jit(solution)/shard_map/all_to_all | solution.py:493
  191.3 0.9 broadcast_in_dim.36.wave_z_ref
  192.2 0.4 copy-done.1
  192.6 14.3 %forward.1 = (f32[32,128,128]{2,1,0:T(8,128)}, f32[2,2,32,128]{3,2,1,0:T(8,128)}) custom-call(f32[4096,128]{1,0:T(8,128)} %bitcast.28, bf16[2,256,256]{2,1,0:T(8,128)(2,1)} %constant.58.clone.cx_ref, bf16[2,128,128]{2,1,0:T(8,128)(2,1)} %constant.59.clone.cy_ref, f32[128,128]{1,0:T(8,128)} %constant.56.clone.plane_ref, ...), custom_call_target="tpu_custom_call" | custom-call | tf_op jit(solution)/shard_map/forward/pallas_call | solution.py:533
  207.0 2.8 %collective-permute-start.8 = (f32[2,2,32,128]{3,2,1,0:T(8,128)}, f32[2,2,32,128]{3,2,1,0:T(8,128)S(1)}, u32[]{:S(2)}, u32[]{:S(2)}) collective-permute-start(f32[2,2,32,128]{3,2,1,0:T(8,128)} %get-tuple-element.8), channel_id=1, source_target_pairs={{0,2},{2,4},{4,6},{6,0},{1,3},{3,5},{5,7},{7,1},{8,10},{10,12},{12... | collective-permute-start | bytes 196616 | tf_op jit(solution)/shard_map/ppermute | solution.py:547
  209.8 0.1 collective-permute-start.9
  209.9 2.9 %collective-permute-start.10 = (f32[2,2,32,128]{3,2,1,0:T(8,128)}, f32[2,2,32,128]{3,2,1,0:T(8,128)S(1)}, u32[]{:S(2)}, u32[]{:S(2)}) collective-permute-start(f32[2,2,32,128]{3,2,1,0:T(8,128)} %get-tuple-element.8), channel_id=1, source_target_pairs={{0,6},{2,0},{4,2},{6,4},{1,7},{3,1},{5,3},{7,5},{8,14},{10,8},{12,... | collective-permute-start | bytes 196616 | tf_op jit(solution)/shard_map/ppermute | solution.py:547
  212.8 1.4 constant_dynamic-slice_fusion
  214.2 1.7 collective-permute-done.9
  215.9 1.6 pad_maximum_fusion.1.rims_ref
  217.4 18.3 %backward.1 = f32[4096,128]{1,0:T(8,128)} custom-call(s32[1]{0:T(128)} %bitcast.place_ref, f32[32,128,128]{2,1,0:T(8,128)} %get-tuple-element.7.spec_ref, f32[4,2,2,32,128]{4,3,2,1,0:T(8,128)} %pad_maximum_fusion.1.rims_ref, f32[2,32,128]{2,1,0:T(8,128)} %get-tuple-element.22.near_ref, f32[2,32,128]{2,1,0:T(8,128)} %get-tuple-element.21.far_ref, ...), custom_call_target="tpu_custom_call" | custom-call | tf_op jit(solution)/shard_map/backward/pallas_call | solution.py:551
  235.8 30.9 %all_to_all.21.lines_ref = f32[8,16,32,128]{3,2,1,0:T(8,128)} all-to-all(f32[8,16,32,128]{3,2,1,0:T(8,128)} %bitcast.29), channel_id=1, replica_groups=mesh['gx'=4,'gy'=4,'gz'=2] {'gx','gz'}, dimensions={0} | all-to-all | bytes 4194304 | tf_op jit(solution)/shard_map/all_to_all | solution.py:563
  266.7 5.7 %last.1 = f32[2,32,64,128]{3,2,1,0:T(8,128)} custom-call(f32[8,16,32,128]{3,2,1,0:T(8,128)} %all_to_all.21.lines_ref, bf16[2,256,256]{2,1,0:T(8,128)(2,1)} %constant.62.clone.cosine_ref), custom_call_target="tpu_custom_call" | custom-call | tf_op jit(solution)/shard_map/last/pallas_call | solution.py:564
  272.4 6.6 %all_to_all.22 = f32[2,1,32,64,128]{4,3,2,1,0:T(8,128)S(1)} all-to-all(f32[2,1,32,64,128]{4,3,2,1,0:T(8,128)} %bitcast.30), channel_id=1, replica_groups=mesh['gx'=4,'gy'=4,'gz'=2] {'gz'}, dimensions={0} | all-to-all | bytes 4194304 | tf_op jit(solution)/shard_map/all_to_all | solution.py:570
  279.0 1.3 copy.44
  (31 shorter events, 0.3 us)
Async XLA Ops:
  1.5 2.2 copy-start.2
  1.5 2.9 %copy-start.3 = (s32[64,64,128]{2,1,0:T(8,128)S(1)}, s32[64,64,128]{2,1,0:T(8,128)}, u32[]{:S(2)}) copy-start(s32[64,64,128]{2,1,0:T(8,128)} %param.18) | copy-start | bytes 6291460
  15.7 11.7 %copy-start = (f32[2,1,2,32,64,128]{5,4,3,2,1,0:T(8,128)}, f32[2,1,2,32,64,128]{5,4,3,2,1,0:T(8,128)S(1)}, u32[]{:S(2)}) copy-start(f32[2,1,2,32,64,128]{5,4,3,2,1,0:T(8,128)S(1)} %all_to_all.20) | copy-start | bytes 12582916
  17.1 47.7 %collective-permute-start = (f32[2,2,9,64,128]{4,3,2,1,0:T(8,128)}, f32[2,2,9,64,128]{4,3,2,1,0:T(8,128)S(1)}, u32[]{:S(2)}, u32[]{:S(2)}) collective-permute-start(f32[2,2,9,64,128]{4,3,2,1,0:T(8,128)} %get-tuple-element.16), channel_id=1, source_target_pairs={{0,1},{2,3},{4,5},{6,7},{1,8},{3,10},{5,12},{7,14},{8,9},{10,11},{... | collective-permute-start | bytes 3538952 | tf_op jit(solution)/shard_map/ppermute | solution.py:447
  19.2 45.6 %collective-permute-start.1 = (f32[2,2,9,64,128]{4,3,2,1,0:T(8,128)S(1)}, f32[2,2,9,64,128]{4,3,2,1,0:T(8,128)S(1)}, u32[]{:S(2)}, u32[]{:S(2)}) collective-permute-start(f32[2,2,9,64,128]{4,3,2,1,0:T(8,128)S(1)} %get-tuple-element.15), channel_id=1, source_target_pairs={{1,0},{3,2},{5,4},{7,6},{8,1},{10,3},{12,5},{14,7},{9,8},{11,10},{... | collective-permute-start | bytes 3538952 | tf_op jit(solution)/shard_map/ppermute | solution.py:447
  20.7 15.2 %collective-permute-start.4 = (f32[2,2,81,128]{3,2,1,0:T(8,128)S(1)}, f32[2,2,81,128]{3,2,1,0:T(8,128)S(1)}, u32[]{:S(2)}, u32[]{:S(2)}) collective-permute-start(f32[2,2,81,128]{3,2,1,0:T(8,128)S(1)} %copy.35), channel_id=1, source_target_pairs={{0,3},{2,5},{4,7},{1,10},{3,12},{5,14},{8,11},{10,13},{12,15},{9,1... | collective-permute-start | bytes 497672 | tf_op jit(solution)/shard_map/ppermute | solution.py:447
  28.9 35.9 %collective-permute-start.2 = (f32[2,2,288,128]{3,2,1,0:T(8,128)}, f32[2,2,288,128]{3,2,1,0:T(8,128)}, u32[]{:S(2)}, u32[]{:S(2)}) collective-permute-start(f32[2,2,288,128]{3,2,1,0:T(8,128)} %copy.31), channel_id=1, source_target_pairs={{0,2},{2,4},{4,6},{1,3},{3,5},{5,7},{8,10},{10,12},{12,14},{9,11},... | collective-permute-start | bytes 1769480 | tf_op jit(solution)/shard_map/ppermute | solution.py:447
  33.6 6.6 %copy-start.9 = (f32[3,256]{1,0:T(4,128)S(1)}, f32[3,256]{1,0:T(4,128)}, u32[]{:S(2)}) copy-start(f32[3,256]{1,0:T(4,128)} %param.20) | copy-start | bytes 9220
  34.5 30.3 %collective-permute-start.3 = (f32[2,2,288,128]{3,2,1,0:T(8,128)}, f32[2,2,288,128]{3,2,1,0:T(8,128)}, u32[]{:S(2)}, u32[]{:S(2)}) collective-permute-start(f32[2,2,288,128]{3,2,1,0:T(8,128)} %copy.33), channel_id=1, source_target_pairs={{2,0},{4,2},{6,4},{3,1},{5,3},{7,5},{10,8},{12,10},{14,12},{11,9},... | collective-permute-start | bytes 1769480 | tf_op jit(solution)/shard_map/ppermute | solution.py:447
  35.9 2.3 copy-start.6
  35.9 0.8 collective-permute-start.5
  36.7 1.5 copy-start.7
  36.7 1.5 collective-permute-start.6
  38.2 0.7 copy-start.8
  38.9 25.9 %collective-permute-start.7 = (f32[2,2,81,128]{3,2,1,0:T(8,128)}, f32[2,2,81,128]{3,2,1,0:T(8,128)}, u32[]{:S(2)}, u32[]{:S(2)}) collective-permute-start(f32[2,2,81,128]{3,2,1,0:T(8,128)} %copy.41), channel_id=1, source_target_pairs={{3,0},{5,2},{7,4},{10,1},{12,3},{14,5},{11,8},{13,10},{15,12},{18,... | collective-permute-start | bytes 497672 | tf_op jit(solution)/shard_map/ppermute | solution.py:447
  64.8 1.1 copy-start.4
  64.8 1.4 copy-start.5
  156.9 7.8 %copy-start.10 = (f32[256]{0:T(256)S(1)}, f32[256]{0:T(256)}, u32[]{:S(2)}) copy-start(f32[256]{0:T(256)} %constant.55.clone) | copy-start | bytes 3076
  156.9 34.4 %all-to-all-start.1 = ((f32[8,16,32,128]{3,2,1,0:T(8,128)}), f32[8,16,32,128]{3,2,1,0:T(8,128)S(1)}, u32[]{:S(2)}, u32[]{:S(2)}) async-start(f32[8,16,32,128]{3,2,1,0:T(8,128)} %diffuse.1), calls=%async_computation.1 | async-start | bytes 4194304 | tf_op jit(solution)/shard_map/all_to_all | solution.py:493
  191.3 1.4 copy-start.1
  207.0 7.3 %collective-permute-start.8 = (f32[2,2,32,128]{3,2,1,0:T(8,128)}, f32[2,2,32,128]{3,2,1,0:T(8,128)S(1)}, u32[]{:S(2)}, u32[]{:S(2)}) collective-permute-start(f32[2,2,32,128]{3,2,1,0:T(8,128)} %get-tuple-element.8), channel_id=1, source_target_pairs={{0,2},{2,4},{4,6},{6,0},{1,3},{3,5},{5,7},{7,1},{8,10},{10,12},{12... | collective-permute-start | bytes 196616 | tf_op jit(solution)/shard_map/ppermute | solution.py:547
  209.8 6.1 %collective-permute-start.9 = (f32[2,2,32,128]{3,2,1,0:T(8,128)}, f32[2,2,32,128]{3,2,1,0:T(8,128)S(1)}, u32[]{:S(2)}, u32[]{:S(2)}) collective-permute-start(f32[2,2,32,128]{3,2,1,0:T(8,128)} %get-tuple-element.8), channel_id=1, source_target_pairs={{0,4},{2,6},{4,0},{6,2},{1,5},{3,7},{5,1},{7,3},{8,12},{10,14},{12... | collective-permute-start | bytes 196616 | tf_op jit(solution)/shard_map/ppermute | solution.py:547
  209.9 6.0 %collective-permute-start.10 = (f32[2,2,32,128]{3,2,1,0:T(8,128)}, f32[2,2,32,128]{3,2,1,0:T(8,128)S(1)}, u32[]{:S(2)}, u32[]{:S(2)}) collective-permute-start(f32[2,2,32,128]{3,2,1,0:T(8,128)} %get-tuple-element.8), channel_id=1, source_target_pairs={{0,6},{2,0},{4,2},{6,4},{1,7},{3,1},{5,3},{7,5},{8,14},{10,8},{12,... | collective-permute-start | bytes 196616 | tf_op jit(solution)/shard_map/ppermute | solution.py:547
